TPU v7x, 32 devices: a whole 2x2x4 slice. The times are simulated.
32 devices in a mesh: tm: 16 (over z, x, core), space: 2 (over y).
Axes of the slice: x: 2, y: 2, z: 4, core: 2. Of those that a mesh axis runs over, the one named last changes fastest.
Arguments:
- fine_nodes: float32 [16, 3, 3, 32, 4096], P('tm', None, None, 'space'), may hold values from -6 to 6
- init_state: float32 [3, 32, 4096], P(None, 'space'), may hold values from -6 to 6
- mean_depth: float32 [32, 4096], P('space'), may hold values from 0.5 to 2
Outputs:
- new_nodes: float32 [16, 3, 3, 32, 4096], P('tm', None, None, 'space')
All inputs are finite; a program needn't handle non-finite values.
Results may differ from a plain program's by a relative error of at most 0.00002.
Values sent between devices are 32-bit elements; how exact they have to be, the bound alone decides.
A program may use at most 64 MiB of HBM per device.

v0:
```python
import functools

import jax
import jax.numpy as jnp
from jax import lax
from jax.experimental import pallas as pl
from jax.experimental.pallas import tpu as pltpu
from jax.sharding import PartitionSpec as P

MESH = pl.DeviceIdType.MESH
DT = 0.3
NU = 1.0 / 3.0
FC = 0.5
LANES = 128
GROUPS = 4


def shift_left(v):
    return pltpu.roll(v, v.shape[1] - 1, 1)


def shift_right(v):
    return pltpu.roll(v, 1, 1)


def shift_up(v):
    return pltpu.roll(v, v.shape[0] - 1, 0)


def shift_down(v):
    return pltpu.roll(v, 1, 0)


def row_terms(h, e, n, depth):
    dn = 0.5 * (depth * n)
    nh, ne, nn, hh = NU * h, NU * e, NU * n, 0.5 * h
    return (nh - dn, ne, nn - hh), (nh + dn, ne, nn + hh)


def column_terms(h, e, n, depth):
    de = 0.5 * (depth * e)
    nh, ne, nn, hh = NU * h, NU * e, NU * n, 0.5 * h
    return (
        shift_left(nh - de) + shift_right(nh + de) - 4.0 * nh,
        shift_left(ne - hh) + shift_right(ne + hh) - 4.0 * ne + FC * n,
        shift_left(nn) + shift_right(nn) - 4.0 * nn - FC * e,
    )


def kernel(
    cfg, u_hbm, init_hbm, depth_hbm, out_ref, u_ref, init_ref, depth_ref,
    s0, g, s1, mid, b, halo_src, dsrc, dep, main, halo, cs, ce, cb, esrc, edst, cin, chalo, chalo_src,
    shift_s, shift_r, edge_s, edge_r, dep_s, dep_r, a2a_s, a2a_r, ret_s, ret_r, fwd_s, fwd_r,
    c_s, c_r, beg_s, beg_r, in_s,
):
    T, SP, RL, NX, W, K, stride, hw, per, nh, NG = cfg
    TG = T // NG
    p, y = lax.axis_index("tm"), lax.axis_index("space")
    me = p * SP + y
    total = T * SP
    block = p // TG
    pb = p - block * TG
    local = pb * SP + y
    mine = local // stride
    is_owner = lax.rem(local, stride) == 0
    even = lax.rem(p, 2) == 0

    def where(flat):
        return (flat // SP, lax.rem(flat, SP))

    barrier = pltpu.get_barrier_semaphore()

    @pl.loop(1, total)
    def _(i):
        pl.semaphore_signal(barrier, inc=1, device_id=where(lax.rem(me + i, total)), device_id_type=MESH)

    loads = [pltpu.make_async_copy(u_hbm.at[0, i], u_ref.at[i], in_s.at[i]) for i in (2, 0, 1)]
    loads.append(pltpu.make_async_copy(depth_hbm, depth_ref, in_s.at[3]))
    loads.append(pltpu.make_async_copy(init_hbm, init_ref, in_s.at[4]))
    for copy in loads:
        copy.start()
    loads[0].wait()
    pl.semaphore_wait(barrier, total - 1)

    shift = pltpu.make_async_remote_copy(
        src_ref=u_ref.at[2], dst_ref=s0, send_sem=shift_s, recv_sem=shift_r,
        device_id=(lax.rem(p + 1, T), y), device_id_type=MESH,
    )

    @pl.when(p < T - 1)
    def _():
        shift.start()

    for copy in loads[1:]:
        copy.wait()

    lane_h = lax.broadcasted_iota(jnp.int32, (RL, LANES), 1)

    def dep_copy(yo):
        return pltpu.make_async_remote_copy(
            src_ref=dsrc.at[yo], dst_ref=dep.at[pl.ds(pl.multiple_of(y * RL, 8), RL)],
            send_sem=dep_s.at[yo], recv_sem=dep_r, device_id=(p, yo), device_id_type=MESH,
        )

    for yo in range(SP):
        flat = pb * SP + yo
        k = flat // stride

        @pl.when(lax.rem(flat, stride) == 0)
        def _():
            here = depth_ref[:, pl.ds(pl.multiple_of(k * W, LANES), W)]
            after = depth_ref[:, pl.ds(pl.multiple_of(lax.rem((k + 1) * W, NX), LANES), LANES)]
            before = depth_ref[:, pl.ds(pl.multiple_of(lax.rem(k * W + NX - LANES, NX), LANES), LANES)]
            dsrc[yo, :, :W] = here
            dsrc[yo, :, W:] = jnp.where(lane_h < LANES // 2, after, before)

            @pl.when(yo != y)
            def _():
                dep_copy(yo).start()

            @pl.when(yo == y)
            def _():
                pltpu.make_async_copy(
                    dsrc.at[yo], dep.at[pl.ds(pl.multiple_of(y * RL, 8), RL)], dep_r
                ).start()

    for f in range(3):
        g[f] = (-7.0 / 24.0) * u_ref[0, f] + (1.0 / 3.0) * u_ref[1, f] - (1.0 / 24.0) * u_ref[2, f]

    @pl.when(p > 0)
    def _():
        shift.wait_recv()

    @pl.when(p == 0)
    def _():
        s0[...] = init_ref[...]

    for f in range(3):
        g[f] = g[f] + 0.5 * s0[f]

    row = lax.broadcasted_iota(jnp.int32, (RL, NX), 0)

    def edge_copy(stage, side):
        to = lax.rem(y + SP - 1, SP) if side == 0 else lax.rem(y + 1, SP)
        return pltpu.make_async_remote_copy(
            src_ref=esrc.at[stage, side], dst_ref=edst.at[stage, side],
            send_sem=edge_s.at[stage, side], recv_sem=edge_r.at[stage, side],
            device_id=(p, to), device_id_type=MESH,
        )

    def rate_of_g(stage):
        up0, _ = row_terms(g[0, 0:1], g[1, 0:1], g[2, 0:1], depth_ref[0:1])
        _, down1 = row_terms(g[0, RL - 1 : RL], g[1, RL - 1 : RL], g[2, RL - 1 : RL], depth_ref[RL - 1 : RL])
        for f in range(3):
            esrc[stage, 0, f] = up0[f]
            esrc[stage, 1, f] = down1[f]
        for side in range(2):
            edge_copy(stage, side).start()
        h, e, n, depth = g[0], g[1], g[2], depth_ref[...]
        rates = column_terms(h, e, n, depth)
        ups, downs = row_terms(h, e, n, depth)
        for side in range(2):
            edge_copy(stage, side).wait_recv()
        return [
            rates[f]
            + jnp.where(row == RL - 1, edst[stage, 0, f], shift_up(ups[f]))
            + jnp.where(row == 0, edst[stage, 1, f], shift_down(downs[f]))
            for f in range(3)
        ]

    rates = rate_of_g(0)
    for f in range(3):
        s1[f] = s0[f] + DT * rates[f]
    for f in range(3):
        g[f] = (
            0.5 * s1[f]
            - (1.0 / 24.0) * u_ref[0, f] - (1.0 / 6.0) * u_ref[1, f] + (5.0 / 24.0) * u_ref[2, f]
        )
    rates = rate_of_g(1)
    first = jnp.where(p == 0, 1.0, 0.0).astype(jnp.float32)
    for f in range(3):
        s2 = s1[f] + DT * rates[f]
        g[f] = (1.0 / 6.0) * s2 + (2.0 / 3.0) * s1[f] + (first - 5.0 / 6.0) * s0[f]
        mid[f] = s1[f] - 0.5 * (s0[f] + s2)
    rates = rate_of_g(2)
    for f in range(3):
        b[f] = first * s0[f] + DT * rates[f]

    slot_of = lax.rem(lane_h + hw, LANES) // (2 * hw)
    for k in range(K):
        lo, hi = ((k + 1) % K) * W, (k * W - LANES) % NX
        packed = [jnp.zeros((RL, LANES), jnp.float32) for _ in range(nh)]
        for f in range(3):
            z = jnp.where(lane_h < LANES // 2, b[f, :, lo : lo + LANES], b[f, :, hi : hi + LANES])
            slot = f % per
            if slot:
                z = pltpu.roll(z, 2 * hw * slot, 1)
            packed[f // per] = jnp.where(slot_of == slot, z, packed[f // per])
        for i in range(nh):
            halo_src[i, :, k * LANES : (k + 1) * LANES] = packed[i]

    my_rows = pl.ds(pl.multiple_of(y * RL, 8), RL)

    def a2a(k):
        ends = (
            (b.at[:, :, pl.ds(pl.multiple_of(k * W, LANES), W)], main.at[pb, :, my_rows]),
            (halo_src.at[:, :, pl.ds(pl.multiple_of(k * LANES, LANES), LANES)], halo.at[pb, :, my_rows]),
        )
        there = [
            pltpu.make_async_remote_copy(
                src_ref=src, dst_ref=dst, send_sem=a2a_s.at[i], recv_sem=a2a_r.at[i, pb],
                device_id=where(block * TG * SP + k * stride), device_id_type=MESH,
            )
            for i, (src, dst) in enumerate(ends)
        ]
        here = [pltpu.make_async_copy(src, dst, a2a_r.at[i, pb]) for i, (src, dst) in enumerate(ends)]
        return there, here

    @pl.loop(0, K)
    def _(i):
        k = lax.rem(mine + i, K)
        there, here = a2a(k)

        @pl.when(k * stride != local)
        def _():
            for copy in there:
                copy.start()

        @pl.when(k * stride == local)
        def _():
            for copy in here:
                copy.start()

    my_tile = pl.ds(pl.multiple_of(mine * W, LANES), W)
    my_group = mine // (K // GROUPS)

    def give_back(t):
        for yo in range(SP):
            src, dst = cs.at[t * SP + yo], ce.at[:, :, my_tile]
            here = jnp.logical_and(t == pb, y == yo)

            @pl.when(jnp.logical_not(here))
            def _():
                pltpu.make_async_remote_copy(
                    src_ref=src, dst_ref=dst, send_sem=ret_s, recv_sem=ret_r.at[my_group],
                    device_id=(block * TG + t, yo), device_id_type=MESH,
                ).start()

            @pl.when(here)
            def _():
                pltpu.make_async_copy(src, dst, ret_r.at[my_group]).start()

    def give_begin(t, src):
        for yo in range(SP):
            dst = cb.at[:, :, my_tile]
            here = jnp.logical_and(t == pb, y == yo)

            @pl.when(jnp.logical_not(here))
            def _():
                pltpu.make_async_remote_copy(
                    src_ref=src.at[yo], dst_ref=dst, send_sem=beg_s.at[t * SP + yo], recv_sem=beg_r,
                    device_id=(block * TG + t, yo), device_id_type=MESH,
                ).start()

            @pl.when(here)
            def _():
                pltpu.make_async_copy(src.at[yo], dst, beg_r).start()

    def give(t):
        give_back(t)

        @pl.when(jnp.logical_and(lax.rem(t, 2) == 1, t < TG - 1))
        def _():
            give_begin(t + 1, cs.at[pl.ds(t * SP, SP)])

    def carry():
        ends = ((cs.at[pl.ds((TG - 1) * SP, SP)], cin), (chalo_src, chalo))
        return [
            pltpu.make_async_remote_copy(
                src_ref=src, dst_ref=dst, send_sem=c_s.at[i], recv_sem=c_r.at[i],
                device_id=(lax.rem(p + TG, T), y), device_id_type=MESH,
            )
            for i, (src, dst) in enumerate(ends)
        ]

    def unpack(tile, f):
        return pltpu.roll(tile, LANES - 2 * hw * (f % per), 1) if f % per else tile

    def whole(ref, sem):
        pltpu.make_async_copy(ref, ref, sem).wait()

    @pl.when(is_owner)
    def _():
        whole(dep, dep_r)
        depth = dep[...]

        def turn(t, cur):
            h, e, n = cur
            rates = column_terms(h, e, n, depth)
            ups, downs = row_terms(h, e, n, depth)
            whole(main.at[t], a2a_r.at[0, t])
            whole(halo.at[t], a2a_r.at[1, t])
            new = []
            for f in range(3):
                window = jnp.concatenate([main[t, f], unpack(halo[t, f // per], f)], axis=1)
                value = window + cur[f] + DT * (rates[f] + shift_up(ups[f]) + shift_down(downs[f]))
                for yo in range(SP):
                    cs[t * SP + yo, f] = value[yo * RL : (yo + 1) * RL, :W]
                new.append(value)

            @pl.when(jnp.logical_and(t > 0, block == NG - 1))
            def _():
                give(t - 1)

            return tuple(new)

        @pl.when(block == 0)
        def _():
            cin[...] = jnp.zeros_like(cin)
            chalo[...] = jnp.zeros_like(chalo)

        @pl.when(block > 0)
        def _():
            for copy in carry():
                copy.wait_recv()
            give_begin(0, cin)

        first_state = tuple(
            jnp.concatenate(
                [jnp.concatenate([cin[yo, f] for yo in range(SP)], axis=0), unpack(chalo[f // per], f)], axis=1
            )
            for f in range(3)
        )
        last = lax.fori_loop(0, TG, turn, first_state)

        @pl.when(block == NG - 1)
        def _():
            give(TG - 1)

        @pl.when(block < NG - 1)
        def _():
            lanes = lax.broadcasted_iota(jnp.int32, (SP * RL, LANES), 1)
            slots = lax.rem(lanes + hw, LANES) // (2 * hw)
            for i in range(nh):
                packed = jnp.zeros((SP * RL, LANES), jnp.float32)
                for f in range(i * per, min(3, (i + 1) * per)):
                    z = last[f][:, W:]
                    if f % per:
                        z = pltpu.roll(z, 2 * hw * (f % per), 1)
                    packed = jnp.where(slots == f % per, z, packed)
                chalo_src[i] = packed
            for copy in carry():
                copy.start()

            @pl.loop(0, TG)
            def _(t):
                give(t)

    width = NX // GROUPS

    def fwd(q):
        cols = pl.ds(q * width, width)
        return pltpu.make_async_remote_copy(
            src_ref=ce.at[:, :, cols], dst_ref=cb.at[:, :, cols],
            send_sem=fwd_s.at[q], recv_sem=fwd_r.at[q], device_id=(lax.rem(p + 1, T), y), device_id_type=MESH,
        )

    for q in range(GROUPS):
        whole(ce.at[:, :, pl.ds(q * width, width)], ret_r.at[q])

        @pl.when(even)
        def _():
            fwd(q).start()

    @pl.when(p == 0)
    def _():
        cb[...] = init_ref[...]

    @pl.when(jnp.logical_and(even, p > 0))
    def _():
        whole(cb, beg_r)

    for q in range(GROUPS):
        @pl.when(jnp.logical_not(even))
        def _():
            fwd(q).wait_recv()

        cols = pl.ds(q * width, width)
        for f in range(3):
            start, end = cb[f, :, cols], ce[f, :, cols]
            out_ref[0, 0, f, :, cols] = start
            out_ref[0, 1, f, :, cols] = mid[f, :, cols] + 0.5 * (start + end)
            out_ref[0, 2, f, :, cols] = end

    @pl.when(p < T - 1)
    def _():
        shift.wait_send()

    @pl.when(even)
    def _():
        for q in range(GROUPS):
            fwd(q).wait_send()

    for stage in range(3):
        for side in range(2):
            edge_copy(stage, side).wait_send()
    for yo in range(SP):
        flat = pb * SP + yo

        @pl.when(jnp.logical_and(lax.rem(flat, stride) == 0, yo != y))
        def _():
            dep_copy(yo).wait_send()

    @pl.when(is_owner)
    def _():
        whole(b.at[:, :, pl.ds(0, (K - 1) * W)], a2a_s.at[0])
        whole(halo_src.at[:, :, pl.ds(0, (K - 1) * LANES)], a2a_s.at[1])
        whole(cs.at[pl.ds(0, TG * SP - 1)], ret_s)

        @pl.when(block < NG - 1)
        def _():
            for copy in carry():
                copy.wait_send()

        for t in range(0, TG, 2):
            for yo in range(SP):
                sent = jnp.logical_not(jnp.logical_and(t == pb, y == yo))
                if t == 0:
                    sent = jnp.logical_and(sent, block > 0)

                @pl.when(sent)
                def _():
                    pltpu.make_async_copy(cin.at[yo], cin.at[yo], beg_s.at[t * SP + yo]).wait()

    @pl.when(jnp.logical_not(is_owner))
    def _():
        whole(b, a2a_s.at[0])
        whole(halo_src, a2a_s.at[1])


def solution(mesh):
    T, SP = mesh.shape["tm"], mesh.shape["space"]

    def per_device(fine_nodes, init_state, mean_depth):
        RL, NX = mean_depth.shape
        NG = 2 if T % 4 == 0 else 1
        members = T // NG * SP
        W = max(LANES, NX // members)
        K = NX // W
        stride = members // K
        hw = 8
        while hw < T:
            hw *= 2
        per = LANES // (2 * hw)
        nh = -(-3 // per)
        cfg = (T, SP, RL, NX, W, K, stride, hw, per, nh, NG)
        f32, dma = jnp.float32, pltpu.SemaphoreType.DMA
        state = pltpu.VMEM((3, RL, NX), f32)
        R = RL * SP
        vmem = pl.BlockSpec(memory_space=pltpu.VMEM)
        return pl.pallas_call(
            functools.partial(kernel, cfg),
            out_shape=pltpu.VMEM(fine_nodes.shape, f32),
            in_specs=[pl.BlockSpec(memory_space=pl.ANY)] * 3,
            out_specs=vmem,
            scratch_shapes=[
                pltpu.VMEM((3, 3, RL, NX), f32), state, pltpu.VMEM((RL, NX), f32),
                state, state, state, state, state,
                pltpu.VMEM((nh, RL, K * LANES), f32),
                pltpu.VMEM((SP, RL, W + LANES), f32),
                pltpu.VMEM((R, W + LANES), f32),
                pltpu.VMEM((T // NG, 3, R, W), f32),
                pltpu.VMEM((T // NG, nh, R, LANES), f32),
                pltpu.VMEM((members, 3, RL, W), f32),
                state, state,
                pltpu.VMEM((3, 2, 3, 1, NX), f32),
                pltpu.VMEM((3, 2, 3, 1, NX), f32),
                pltpu.VMEM((SP, 3, RL, W), f32),
                pltpu.VMEM((nh, R, LANES), f32),
                pltpu.VMEM((nh, R, LANES), f32),
                dma, dma, dma((3, 2)), dma((3, 2)), dma((SP,)), dma, dma((2,)), dma((2, T // NG)),
                dma, dma((GROUPS,)), dma((GROUPS,)), dma((GROUPS,)),
                dma((2,)), dma((2,)), dma((members,)), dma, dma((5,)),
            ],
            compiler_params=pltpu.CompilerParams(
                collective_id=0, has_side_effects=True, vmem_limit_bytes=60 * 1024 * 1024
            ),
        )(fine_nodes, init_state, mean_depth)

    return jax.shard_map(
        per_device,
        mesh=mesh,
        in_specs=(P("tm", None, None, "space", None), P(None, "space", None), P("space", None)),
        out_specs=P("tm", None, None, "space", None),
        check_vma=False,
    )
```

profile of v0, /device:TPU:27, one launch (start us, length us, event | category | flops | bytes accessed | tf_op | source)
XLA Modules:
  0.0 64.1 jit_solution(2155460267462930013)
XLA Ops:
  0.0 62.6 %shard_map.37 = f32[1,3,3,16,4096]{4,3,2,1,0:T(8,128)S(1)} custom-call(f32[1,3,3,16,4096]{4,3,2,1,0:T(8,128)} %u_hbm.1, f32[3,16,4096]{2,1,0:T(8,128)} %init_hbm.1, f32[16,4096]{1,0:T(8,128)} %depth_hbm.1), custom_call_target="tpu_custom_call" | custom-call | tf_op jit(solution)/shard_map/pallas_call | solution.py:461
  62.6 1.4 %copy.5 = f32[1,3,3,16,4096]{4,3,2,1,0:T(8,128)} copy(f32[1,3,3,16,4096]{4,3,2,1,0:T(8,128)S(1)} %shard_map.37) | data formatting | bytes 4718592
where the time goes:
time: 64.2 us; the launch traced here: 64.1 us
  Pallas kernels  62.6 us (98%)
  local copies, waits for them, and re-layouts  1.41 us (2%)
    pallas_call x1, Pallas kernels, per_device(): pl.pallas_call(functools.partial(kernel, cfg), out_shape=pltpu.VMEM(fine_...  62.6 us
    unnamed x1, local copies, waits for them, and re-layouts  1.41 us

commit v1 on v0

--- a/solution.py
+++ b/solution.py
@@ -49,8 +49,8 @@
 
 def kernel(
     cfg, u_hbm, init_hbm, depth_hbm, out_ref, u_ref, init_ref, depth_ref,
-    s0, g, s1, mid, b, halo_src, dsrc, dep, main, halo, cs, ce, cb, esrc, edst, cin, chalo, chalo_src,
-    shift_s, shift_r, edge_s, edge_r, dep_s, dep_r, a2a_s, a2a_r, ret_s, ret_r, fwd_s, fwd_r,
+    s0, g, s1, mid, b, halo_src, dsrc, dep, isrc, ini, main, halo, cs, ce, cb, esrc, edst, cin, chalo, chalo_src, state,
+    shift_s, shift_r, edge_s, edge_r, dep_s, dep_r, ini_s, ini_r, a2a_s, a2a_r, ret_s, ret_r, fwd_s, fwd_r,
     c_s, c_r, beg_s, beg_r, in_s,
 ):
     T, SP, RL, NX, W, K, stride, hw, per, nh, NG = cfg
@@ -102,6 +102,12 @@
             send_sem=dep_s.at[yo], recv_sem=dep_r, device_id=(p, yo), device_id_type=MESH,
         )
 
+    def ini_copy(yo):
+        return pltpu.make_async_remote_copy(
+            src_ref=isrc.at[yo], dst_ref=ini.at[:, pl.ds(pl.multiple_of(y * RL, 8), RL)],
+            send_sem=ini_s.at[yo], recv_sem=ini_r, device_id=(p, yo), device_id_type=MESH,
+        )
+
     for yo in range(SP):
         flat = pb * SP + yo
         k = flat // stride
@@ -122,6 +128,24 @@
             def _():
                 pltpu.make_async_copy(
                     dsrc.at[yo], dep.at[pl.ds(pl.multiple_of(y * RL, 8), RL)], dep_r
+                ).start()
+
+        @pl.when(jnp.logical_and(lax.rem(flat, stride) == 0, block == 0))
+        def _():
+            for f in range(3):
+                after = init_ref[f, :, pl.ds(pl.multiple_of(lax.rem((k + 1) * W, NX), LANES), LANES)]
+                before = init_ref[f, :, pl.ds(pl.multiple_of(lax.rem(k * W + NX - LANES, NX), LANES), LANES)]
+                isrc[yo, f, :, :W] = init_ref[f, :, pl.ds(pl.multiple_of(k * W, LANES), W)]
+                isrc[yo, f, :, W:] = jnp.where(lane_h < LANES // 2, after, before)
+
+            @pl.when(yo != y)
+            def _():
+                ini_copy(yo).start()
+
+            @pl.when(yo == y)
+            def _():
+                pltpu.make_async_copy(
+                    isrc.at[yo], ini.at[:, pl.ds(pl.multiple_of(y * RL, 8), RL)], ini_r
                 ).start()
 
     for f in range(3):
@@ -177,14 +201,10 @@
             - (1.0 / 24.0) * u_ref[0, f] - (1.0 / 6.0) * u_ref[1, f] + (5.0 / 24.0) * u_ref[2, f]
         )
     rates = rate_of_g(1)
-    first = jnp.where(p == 0, 1.0, 0.0).astype(jnp.float32)
     for f in range(3):
         s2 = s1[f] + DT * rates[f]
-        g[f] = (1.0 / 6.0) * s2 + (2.0 / 3.0) * s1[f] + (first - 5.0 / 6.0) * s0[f]
+        b[f] = (1.0 / 6.0) * s2 + (2.0 / 3.0) * s1[f] - (5.0 / 6.0) * s0[f]
         mid[f] = s1[f] - 0.5 * (s0[f] + s2)
-    rates = rate_of_g(2)
-    for f in range(3):
-        b[f] = first * s0[f] + DT * rates[f]
 
     slot_of = lax.rem(lane_h + hw, LANES) // (2 * hw)
     for k in range(K):
@@ -295,15 +315,16 @@
         depth = dep[...]
 
         def turn(t, cur):
-            h, e, n = cur
+            whole(main.at[t], a2a_r.at[0, t])
+            whole(halo.at[t], a2a_r.at[1, t])
+            h, e, n = (
+                cur[f] + jnp.concatenate([main[t, f], unpack(halo[t, f // per], f)], axis=1) for f in range(3)
+            )
             rates = column_terms(h, e, n, depth)
             ups, downs = row_terms(h, e, n, depth)
-            whole(main.at[t], a2a_r.at[0, t])
-            whole(halo.at[t], a2a_r.at[1, t])
             new = []
             for f in range(3):
-                window = jnp.concatenate([main[t, f], unpack(halo[t, f // per], f)], axis=1)
-                value = window + cur[f] + DT * (rates[f] + shift_up(ups[f]) + shift_down(downs[f]))
+                value = cur[f] + DT * (rates[f] + shift_up(ups[f]) + shift_down(downs[f]))
                 for yo in range(SP):
                     cs[t * SP + yo, f] = value[yo * RL : (yo + 1) * RL, :W]
                 new.append(value)
@@ -316,22 +337,20 @@
 
         @pl.when(block == 0)
         def _():
-            cin[...] = jnp.zeros_like(cin)
-            chalo[...] = jnp.zeros_like(chalo)
+            whole(ini, ini_r)
+            state[...] = ini[...]
 
         @pl.when(block > 0)
         def _():
             for copy in carry():
                 copy.wait_recv()
             give_begin(0, cin)
-
-        first_state = tuple(
-            jnp.concatenate(
-                [jnp.concatenate([cin[yo, f] for yo in range(SP)], axis=0), unpack(chalo[f // per], f)], axis=1
-            )
-            for f in range(3)
-        )
-        last = lax.fori_loop(0, TG, turn, first_state)
+            for f in range(3):
+                for yo in range(SP):
+                    state[f, yo * RL : (yo + 1) * RL, :W] = cin[yo, f]
+                state[f, :, W:] = unpack(chalo[f // per], f)
+
+        last = lax.fori_loop(0, TG, turn, tuple(state[f] for f in range(3)))
 
         @pl.when(block == NG - 1)
         def _():
@@ -401,7 +420,7 @@
         for q in range(GROUPS):
             fwd(q).wait_send()
 
-    for stage in range(3):
+    for stage in range(2):
         for side in range(2):
             edge_copy(stage, side).wait_send()
     for yo in range(SP):
@@ -410,6 +429,10 @@
         @pl.when(jnp.logical_and(lax.rem(flat, stride) == 0, yo != y))
         def _():
             dep_copy(yo).wait_send()
+
+            @pl.when(block == 0)
+            def _():
+                ini_copy(yo).wait_send()
 
     @pl.when(is_owner)
     def _():
@@ -469,16 +492,19 @@
                 pltpu.VMEM((nh, RL, K * LANES), f32),
                 pltpu.VMEM((SP, RL, W + LANES), f32),
                 pltpu.VMEM((R, W + LANES), f32),
+                pltpu.VMEM((SP, 3, RL, W + LANES), f32),
+                pltpu.VMEM((3, R, W + LANES), f32),
                 pltpu.VMEM((T // NG, 3, R, W), f32),
                 pltpu.VMEM((T // NG, nh, R, LANES), f32),
                 pltpu.VMEM((members, 3, RL, W), f32),
                 state, state,
-                pltpu.VMEM((3, 2, 3, 1, NX), f32),
-                pltpu.VMEM((3, 2, 3, 1, NX), f32),
+                pltpu.VMEM((2, 2, 3, 1, NX), f32),
+                pltpu.VMEM((2, 2, 3, 1, NX), f32),
                 pltpu.VMEM((SP, 3, RL, W), f32),
                 pltpu.VMEM((nh, R, LANES), f32),
                 pltpu.VMEM((nh, R, LANES), f32),
-                dma, dma, dma((3, 2)), dma((3, 2)), dma((SP,)), dma, dma((2,)), dma((2, T // NG)),
+                pltpu.VMEM((3, R, W + LANES), f32),
+                dma, dma, dma((2, 2)), dma((2, 2)), dma((SP,)), dma, dma((SP,)), dma, dma((2,)), dma((2, T // NG)),
                 dma, dma((GROUPS,)), dma((GROUPS,)), dma((GROUPS,)),
                 dma((2,)), dma((2,)), dma((members,)), dma, dma((5,)),
             ],

time: 64.2 us -> 60.2 us (0.938)
  Pallas kernels: 62.6 us -> 58.7 us
    pallas_call x1, Pallas kernels: 62.6 us -> 58.7 us  [per_device(): pl.pallas_call(functools.partial(kernel, cfg), out_shape=pltpu.VMEM(fine_...]
where the time goes in v1:
time: 60.2 us; the launch traced here: 60.1 us
  Pallas kernels  58.7 us (98%)
  local copies, waits for them, and re-layouts  1.41 us (2%)
    pallas_call x1, Pallas kernels, per_device(): pl.pallas_call(functools.partial(kernel, cfg), out_shape=pltpu.VMEM(fine_...  58.7 us
    unnamed x1, local copies, waits for them, and re-layouts  1.41 us

profile of v1, /device:TPU:27, one launch (start us, length us, event | category | flops | bytes accessed | tf_op | source)
XLA Modules:
  0.0 60.1 jit_solution(5526092533975766866)
XLA Ops:
  0.0 58.7 %shard_map.37 = f32[1,3,3,16,4096]{4,3,2,1,0:T(8,128)S(1)} custom-call(f32[1,3,3,16,4096]{4,3,2,1,0:T(8,128)} %u_hbm.1, f32[3,16,4096]{2,1,0:T(8,128)} %init_hbm.1, f32[16,4096]{1,0:T(8,128)} %depth_hbm.1), custom_call_target="tpu_custom_call" | custom-call | tf_op jit(solution)/shard_map/pallas_call | solution.py:484
  58.7 1.4 %copy.5 = f32[1,3,3,16,4096]{4,3,2,1,0:T(8,128)} copy(f32[1,3,3,16,4096]{4,3,2,1,0:T(8,128)S(1)} %shard_map.37) | data formatting | bytes 4718592

commit v2 on v0

v2 whole, which is shorter than its diff:
```python
import functools

import jax
import jax.numpy as jnp
from jax import lax
from jax.experimental import pallas as pl
from jax.experimental.pallas import tpu as pltpu
from jax.sharding import PartitionSpec as P

MESH = pl.DeviceIdType.MESH
DT = 0.3
NU = 1.0 / 3.0
FC = 0.5
DIFF = DT * NU
HALF = DT * 0.5
TURN = DT * FC
LANES = 128
SUB = 8
CHUNKS = 4
GROUPS = 4


def shift_left(v):
    return pltpu.roll(v, v.shape[1] - 1, 1)


def shift_right(v):
    return pltpu.roll(v, 1, 1)


def shift_up(v):
    return pltpu.roll(v, v.shape[0] - 1, 0)


def shift_down(v):
    return pltpu.roll(v, 1, 0)


def row_terms(h, e, n, depth):
    dn = depth * n
    nh, ne, nn, hh = DIFF * h, DIFF * e, DIFF * n, HALF * h
    return (nh - dn, ne, nn - hh), (nh + dn, ne, nn + hh)


def column_terms(h, e, n, depth):
    de = depth * e
    nh, ne, nn, hh = DIFF * h, DIFF * e, DIFF * n, HALF * h
    return (
        shift_left(nh - de) + shift_right(nh + de) - 4.0 * nh,
        shift_left(ne - hh) + shift_right(ne + hh) - 4.0 * ne + TURN * n,
        shift_left(nn) + shift_right(nn) - 4.0 * nn - TURN * e,
    )


def periodic_rate(state, depth):
    rates = column_terms(*state, depth)
    ups, downs = row_terms(*state, depth)
    return [rates[f] + shift_up(ups[f]) + shift_down(downs[f]) for f in range(3)]


def kernel(
    cfg, u_hbm, init_hbm, depth_hbm, out_ref, u_ref, init_ref, depth_ref,
    w, s0, g, s1, mid, b, halo_src, rsrc, rdst, dhsrc, dhdst, dsrc, dep, isrc, ini, main, halo, cs, ce, cb,
    esrc, edst, eo, redge, cin, chalo, chalo_src, state,
    shift_s, shift_r, rel_s, rel_r, dh_s, dh_r, edge_s, edge_r, dep_s, dep_r, ini_s, ini_r, a2a_s, a2a_r, ret_s, ret_r,
    fwd_s, fwd_r, c_s, c_r, beg_s, beg_r, in_s,
):
    T, SP, RL, NX, W, K, stride, hw, per, nh, NG, NC = cfg
    TG = T // NG
    WC = NX // NC
    tpc = K // NC
    sides = 1 if SP == 2 else 2
    p, y = lax.axis_index("tm"), lax.axis_index("space")
    me = p * SP + y
    total = T * SP
    block = p // TG
    pb = p - block * TG
    local = pb * SP + y
    is_owner = lax.rem(local, stride) == 0
    even = lax.rem(p, 2) == 0
    odd = jnp.logical_not(even)
    late = jnp.logical_and(even, p > 0)

    def tile_of(j):
        return lax.rem(j, NC) * tpc + j // NC

    def owner_of(k):
        return lax.rem(k, tpc) * NC + k // tpc

    mine = tile_of(local // stride)

    def where(flat):
        return (flat // SP, lax.rem(flat, SP))

    def row_neighbour(side):
        return lax.rem(y + SP - 1, SP) if side == 0 else lax.rem(y + 1, SP)

    barrier = pltpu.get_barrier_semaphore()

    @pl.loop(1, total)
    def _(i):
        pl.semaphore_signal(barrier, inc=1, device_id=where(lax.rem(me + i, total)), device_id_type=MESH)

    loads = [pltpu.make_async_copy(u_hbm.at[0, i], u_ref.at[i], in_s.at[i]) for i in (2, 0, 1)]
    loads.append(pltpu.make_async_copy(depth_hbm, depth_ref, in_s.at[3]))
    loads.append(pltpu.make_async_copy(init_hbm, init_ref, in_s.at[4]))
    for copy in loads:
        copy.start()
    loads[0].wait()
    pl.semaphore_wait(barrier, total - 1)

    def chunk(c):
        return pl.ds(c * WC, WC)

    def shift(c, dst):
        return pltpu.make_async_remote_copy(
            src_ref=u_ref.at[2, :, :, chunk(c)], dst_ref=dst.at[:, :, chunk(c)],
            send_sem=shift_s.at[c], recv_sem=shift_r.at[c],
            device_id=(lax.rem(p + 1, T), y), device_id_type=MESH,
        )

    @pl.when(jnp.logical_and(odd, p < T - 1))
    def _():
        for c in range(NC):
            shift(c, w).start()

    @pl.when(even)
    def _():
        for c in range(NC):
            shift(c, s0).start()

    for copy in loads[1:]:
        copy.wait()

    depth_ref[...] = HALF * depth_ref[...]

    lane_h = lax.broadcasted_iota(jnp.int32, (RL, LANES), 1)
    row8 = lax.broadcasted_iota(jnp.int32, (SUB, NX), 0)
    row8c = lax.broadcasted_iota(jnp.int32, (SUB, WC), 0)

    def margin(ref, c):
        after = ref[:, pl.ds((c + 1) % NC * WC, LANES)]
        before = ref[:, pl.ds((c * WC - LANES) % NX, LANES)]
        lanes = lax.broadcasted_iota(jnp.int32, after.shape, 1)
        return jnp.where(lanes < LANES // 2, after, before)

    def window(ref, c):
        return jnp.concatenate([ref[:, chunk(c)], margin(ref, c)], axis=1)

    def depth_halo(side):
        return pltpu.make_async_remote_copy(
            src_ref=dhsrc, dst_ref=dhdst.at[side], send_sem=dh_s.at[side], recv_sem=dh_r.at[side],
            device_id=(p, row_neighbour(side)), device_id_type=MESH,
        )

    @pl.when(late)
    def _():
        dhsrc[...] = jnp.where(row8 < SUB // 2, depth_ref[:SUB], depth_ref[RL - SUB :])
        for side in range(sides):
            depth_halo(side).start()
        s0[...] = jnp.zeros_like(s0)

    @pl.when(p == 0)
    def _():
        s0[...] = init_ref[...]

    @pl.when(odd)
    def _():
        for c in range(NC):
            shift(c, s0).wait_recv()

    row = lax.broadcasted_iota(jnp.int32, (RL, NX), 0)

    def edge_copy(stage, side):
        return pltpu.make_async_remote_copy(
            src_ref=esrc.at[stage, side], dst_ref=edst.at[stage, side],
            send_sem=edge_s.at[stage, side], recv_sem=edge_r.at[stage, side],
            device_id=(p, row_neighbour(side)), device_id_type=MESH,
        )

    def send_edges(stage, rows_of):
        top, bottom = rows_of(0), rows_of(RL - 1)
        up0, _ = row_terms(*top, depth_ref[0:1])
        _, down1 = row_terms(*bottom, depth_ref[RL - 1 : RL])
        for f in range(3):
            esrc[stage, 0, f] = up0[f]
            esrc[stage, 1, f] = down1[f]
        for side in range(2):
            edge_copy(stage, side).start()

    def rate_of_g(stage, between):
        between()
        h, e, n, depth = g[0], g[1], g[2], depth_ref[...]
        rates = column_terms(h, e, n, depth)
        ups, downs = row_terms(h, e, n, depth)
        for side in range(2):
            edge_copy(stage, side).wait_recv()
        return [
            rates[f]
            + jnp.where(row == RL - 1, edst[stage, 0, f], shift_up(ups[f]))
            + jnp.where(row == 0, edst[stage, 1, f], shift_down(downs[f]))
            for f in range(3)
        ]

    def relay(c, side):
        return pltpu.make_async_remote_copy(
            src_ref=rsrc.at[:, :, chunk(c)], dst_ref=rdst.at[side, :, :, chunk(c)],
            send_sem=rel_s.at[side, c], recv_sem=rel_r.at[side, c],
            device_id=(p, row_neighbour(side)), device_id_type=MESH,
        )

    def relay_chunks(chunks):
        @pl.when(late)
        def _():
            for c in chunks:
                shift(c, w).wait_recv()
                for f in range(3):
                    rsrc[f, :, chunk(c)] = jnp.where(row8c < SUB // 2, w[f, :SUB, chunk(c)], w[f, RL - SUB :, chunk(c)])
                for side in range(sides):
                    relay(c, side).start()

    def first_g(rows, f):
        return (
            (-7.0 / 24.0) * u_ref[0, f, rows] + (1.0 / 3.0) * u_ref[1, f, rows] - (1.0 / 24.0) * u_ref[2, f, rows]
            + 0.5 * s0[f, rows]
        )

    send_edges(0, lambda r: [first_g(slice(r, r + 1), f) for f in range(3)])
    for f in range(3):
        g[f] = first_g(slice(0, RL), f)

    def dep_copy(yo):
        return pltpu.make_async_remote_copy(
            src_ref=dsrc.at[yo], dst_ref=dep.at[pl.ds(pl.multiple_of(y * RL, 8), RL)],
            send_sem=dep_s.at[yo], recv_sem=dep_r, device_id=(p, yo), device_id_type=MESH,
        )

    def ini_copy(yo):
        return pltpu.make_async_remote_copy(
            src_ref=isrc.at[yo], dst_ref=ini.at[:, pl.ds(pl.multiple_of(y * RL, 8), RL)],
            send_sem=ini_s.at[yo], recv_sem=ini_r, device_id=(p, yo), device_id_type=MESH,
        )

    def owner_tables():
        for yo in range(SP):
            flat = pb * SP + yo
            k = tile_of(flat // stride)
            at_k = pl.ds(pl.multiple_of(k * W, LANES), W)
            at_after = pl.ds(pl.multiple_of(lax.rem((k + 1) * W, NX), LANES), LANES)
            at_before = pl.ds(pl.multiple_of(lax.rem(k * W + NX - LANES, NX), LANES), LANES)

            @pl.when(lax.rem(flat, stride) == 0)
            def _():
                dsrc[yo, :, :W] = depth_ref[:, at_k]
                dsrc[yo, :, W:] = jnp.where(lane_h < LANES // 2, depth_ref[:, at_after], depth_ref[:, at_before])

                @pl.when(yo != y)
                def _():
                    dep_copy(yo).start()

                @pl.when(yo == y)
                def _():
                    pltpu.make_async_copy(
                        dsrc.at[yo], dep.at[pl.ds(pl.multiple_of(y * RL, 8), RL)], dep_r
                    ).start()

            @pl.when(jnp.logical_and(lax.rem(flat, stride) == 0, block == 0))
            def _():
                for f in range(3):
                    isrc[yo, f, :, :W] = init_ref[f, :, at_k]
                    isrc[yo, f, :, W:] = jnp.where(
                        lane_h < LANES // 2, init_ref[f, :, at_after], init_ref[f, :, at_before]
                    )

                @pl.when(yo != y)
                def _():
                    ini_copy(yo).start()

                @pl.when(yo == y)
                def _():
                    pltpu.make_async_copy(
                        isrc.at[yo], ini.at[:, pl.ds(pl.multiple_of(y * RL, 8), RL)], ini_r
                    ).start()

    def between_zero():
        owner_tables()
        relay_chunks(range(0, NC // 4))

    rates = rate_of_g(0, between_zero)
    for f in range(3):
        s1[f] = s0[f] + rates[f]
    for f in range(3):
        g[f] = (
            0.5 * s1[f]
            - (1.0 / 24.0) * u_ref[0, f] - (1.0 / 6.0) * u_ref[1, f] + (5.0 / 24.0) * u_ref[2, f]
        )
    send_edges(1, lambda r: [g[f, r : r + 1] for f in range(3)])
    rates = rate_of_g(1, lambda: relay_chunks(range(NC // 4, NC)))
    for f in range(3):
        s2 = s1[f] + rates[f]
        b[f] = (1.0 / 6.0) * s2 + (2.0 / 3.0) * s1[f] - (5.0 / 6.0) * s0[f]
        mid[f] = s1[f] - 0.5 * (s0[f] + s2)

    my_rows = pl.ds(pl.multiple_of(y * RL, 8), RL)

    def a2a(i, k):
        j = owner_of(k)
        if i == 0:
            src, dst = b.at[:, :, pl.ds(pl.multiple_of(k * W, LANES), W)], main.at[pb, :, my_rows]
        else:
            src, dst = halo_src.at[:, :, pl.ds(pl.multiple_of(k * LANES, LANES), LANES)], halo.at[pb, :, my_rows]

        @pl.when(j * stride != local)
        def _():
            pltpu.make_async_remote_copy(
                src_ref=src, dst_ref=dst, send_sem=a2a_s.at[i], recv_sem=a2a_r.at[i, pb],
                device_id=where(block * TG * SP + j * stride), device_id_type=MESH,
            ).start()

        @pl.when(j * stride == local)
        def _():
            pltpu.make_async_copy(src, dst, a2a_r.at[i, pb]).start()

    def extended(own, tile):
        return jnp.concatenate([own, tile], axis=0)

    def late_chunk(c):
        if sides == 1:
            tiles = [window(rdst.at[0, f], c) for f in range(3)]
            depth_tile = window(dhdst.at[0], c)
        else:
            rows8 = lax.broadcasted_iota(jnp.int32, (SUB, WC + LANES), 0)
            tiles = [
                jnp.where(rows8 < SUB // 2, window(rdst.at[0, f], c), window(rdst.at[1, f], c)) for f in range(3)
            ]
            depth_tile = jnp.where(rows8 < SUB // 2, window(dhdst.at[0], c), window(dhdst.at[1], c))
        depth = extended(window(depth_ref, c), depth_tile)
        start = [extended(window(w.at[f], c), tiles[f]) for f in range(3)]
        once = periodic_rate(start, depth)
        twice = periodic_rate(once, depth)
        for f in range(3):
            one, two = once[f][:RL, :WC], twice[f][:RL, :WC]
            b[f, :, chunk(c)] = b[f, :, chunk(c)] + (0.5 * one + (1.0 / 24.0) * two)
            mid[f, :, chunk(c)] = mid[f, :, chunk(c)] - 0.125 * two

        @pl.loop(0, tpc)
        def _(i):
            a2a(0, c * tpc + lax.rem(mine + i, tpc))

    @pl.when(late)
    def _():
        for side in range(sides):
            depth_halo(side).wait_recv()
        arrived = 0
        for step in range(1, NC + 1):
            c = step % NC
            while arrived < min(step + 2, NC):
                for side in range(sides):
                    relay(arrived, side).wait_recv()
                arrived += 1
            late_chunk(c)

    @pl.when(jnp.logical_not(late))
    def _():
        @pl.loop(0, K)
        def _(i):
            a2a(0, lax.rem(mine + i, K))

    slot_of = lax.rem(lane_h + hw, LANES) // (2 * hw)
    for k in range(K):
        lo, hi = ((k + 1) % K) * W, (k * W - LANES) % NX
        packed = [jnp.zeros((RL, LANES), jnp.float32) for _ in range(nh)]
        for f in range(3):
            z = jnp.where(lane_h < LANES // 2, b[f, :, lo : lo + LANES], b[f, :, hi : hi + LANES])
            slot = f % per
            if slot:
                z = pltpu.roll(z, 2 * hw * slot, 1)
            packed[f // per] = jnp.where(slot_of == slot, z, packed[f // per])
        for i in range(nh):
            halo_src[i, :, k * LANES : (k + 1) * LANES] = packed[i]

    @pl.loop(0, K)
    def _(i):
        a2a(1, lax.rem(mine + i, K))

    my_tile = pl.ds(pl.multiple_of(mine * W, LANES), W)
    my_group = mine // (K // GROUPS)

    def give_edges(t):
        for yo in range(SP):
            src, dst = eo.at[t * SP + yo], redge.at[:, :, :, my_tile]
            here = jnp.logical_and(t == pb, y == yo)

            @pl.when(jnp.logical_not(here))
            def _():
                pltpu.make_async_remote_copy(
                    src_ref=src, dst_ref=dst, send_sem=ret_s, recv_sem=ret_r.at[my_group],
                    device_id=(block * TG + t, yo), device_id_type=MESH,
                ).start()

            @pl.when(here)
            def _():
                pltpu.make_async_copy(src, dst, ret_r.at[my_group]).start()

    def give_begin(t, src):
        for yo in range(SP):
            dst = cb.at[:, :, my_tile]
            here = jnp.logical_and(t == pb, y == yo)

            @pl.when(jnp.logical_not(here))
            def _():
                pltpu.make_async_remote_copy(
                    src_ref=src.at[yo], dst_ref=dst, send_sem=beg_s.at[t * SP + yo], recv_sem=beg_r.at[my_group],
                    device_id=(block * TG + t, yo), device_id_type=MESH,
                ).start()

            @pl.when(here)
            def _():
                pltpu.make_async_copy(src.at[yo], dst, beg_r.at[my_group]).start()

    def give(t):
        give_edges(t)

        @pl.when(jnp.logical_and(lax.rem(t, 2) == 1, t < TG - 1))
        def _():
            give_begin(t + 1, cs.at[pl.ds(t * SP, SP)])

    def carry():
        ends = ((cs.at[pl.ds((TG - 1) * SP, SP)], cin), (chalo_src, chalo))
        return [
            pltpu.make_async_remote_copy(
                src_ref=src, dst_ref=dst, send_sem=c_s.at[i], recv_sem=c_r.at[i],
                device_id=(lax.rem(p + TG, T), y), device_id_type=MESH,
            )
            for i, (src, dst) in enumerate(ends)
        ]

    def unpack(tile, f):
        return pltpu.roll(tile, LANES - 2 * hw * (f % per), 1) if f % per else tile

    def whole(ref, sem):
        pltpu.make_async_copy(ref, ref, sem).wait()

    R = SP * RL

    @pl.when(is_owner)
    def _():
        whole(dep, dep_r)
        depth = dep[...]

        def turn(t, cur):
            whole(main.at[t], a2a_r.at[0, t])
            whole(halo.at[t], a2a_r.at[1, t])
            h, e, n = (
                cur[f] + jnp.concatenate([main[t, f], unpack(halo[t, f // per], f)], axis=1) for f in range(3)
            )
            rates = column_terms(h, e, n, depth)
            ups, downs = row_terms(h, e, n, depth)
            new = []
            for f in range(3):
                value = cur[f] + (rates[f] + shift_up(ups[f]) + shift_down(downs[f]))
                for yo in range(SP):
                    cs[t * SP + yo, f] = value[yo * RL : (yo + 1) * RL, :W]
                    below, above = (yo + 1) * RL % R, (yo * RL - 1) % R
                    eo[t * SP + yo, 0, f] = ups[f][below : below + 1, :W]
                    eo[t * SP + yo, 1, f] = downs[f][above : above + 1, :W]
                new.append(value)

            @pl.when(jnp.logical_and(t > 0, block == NG - 1))
            def _():
                give(t - 1)

            return tuple(new)

        @pl.when(block == 0)
        def _():
            whole(ini, ini_r)
            state[...] = ini[...]

        @pl.when(block > 0)
        def _():
            for copy in carry():
                copy.wait_recv()
            give_begin(0, cin)
            for f in range(3):
                for yo in range(SP):
                    state[f, yo * RL : (yo + 1) * RL, :W] = cin[yo, f]
                state[f, :, W:] = unpack(chalo[f // per], f)

        last = lax.fori_loop(0, TG, turn, tuple(state[f] for f in range(3)))

        @pl.when(block == NG - 1)
        def _():
            give(TG - 1)

        @pl.when(block < NG - 1)
        def _():
            lanes = lax.broadcasted_iota(jnp.int32, (SP * RL, LANES), 1)
            slots = lax.rem(lanes + hw, LANES) // (2 * hw)
            for i in range(nh):
                packed = jnp.zeros((SP * RL, LANES), jnp.float32)
                for f in range(i * per, min(3, (i + 1) * per)):
                    z = last[f][:, W:]
                    if f % per:
                        z = pltpu.roll(z, 2 * hw * (f % per), 1)
                    packed = jnp.where(slots == f % per, z, packed)
                chalo_src[i] = packed
            for copy in carry():
                copy.start()

            @pl.loop(0, TG)
            def _(t):
                give(t)

    width = NX // GROUPS

    def fwd(q):
        cols = pl.ds(q * width, width)
        return pltpu.make_async_remote_copy(
            src_ref=ce.at[:, :, cols], dst_ref=cb.at[:, :, cols],
            send_sem=fwd_s.at[q], recv_sem=fwd_r.at[q], device_id=(lax.rem(p + 1, T), y), device_id_type=MESH,
        )

    for q in range(GROUPS):
        whole(redge.at[:, :, :, pl.ds(q * width, width)], ret_r.at[q])

    @pl.when(p == 0)
    def _():
        cb[...] = init_ref[...]

    @pl.when(late)
    def _():
        for q in range(GROUPS):
            whole(cb.at[:, :, pl.ds(q * width, width)], beg_r.at[q])

    rowc = lax.broadcasted_iota(jnp.int32, (RL, WC), 0)

    def finish(q):
        cols = chunk(q)
        v = [window(cb.at[f], q) + window(b.at[f], q) for f in range(3)]
        rates = column_terms(*v, window(depth_ref, q))
        ups, downs = row_terms(*(v[f][:, :WC] for f in range(3)), depth_ref[:, cols])
        for f in range(3):
            start = cb[f, :, cols]
            end = (
                start + rates[f][:, :WC]
                + jnp.where(rowc == RL - 1, redge[0, f, :, cols], shift_up(ups[f]))
                + jnp.where(rowc == 0, redge[1, f, :, cols], shift_down(downs[f]))
            )
            ce[f, :, cols] = end
            out_ref[0, 0, f, :, cols] = start
            out_ref[0, 1, f, :, cols] = mid[f, :, cols] + 0.5 * (start + end)
            out_ref[0, 2, f, :, cols] = end

    @pl.when(even)
    def _():
        for q in range(NC):
            finish(q)
            fwd(q).start()

    @pl.when(odd)
    def _():
        arrived = 0
        for step in range(1, NC + 1):
            while arrived < min(step + 2, NC):
                fwd(arrived).wait_recv()
                arrived += 1
            finish(step % NC)

    @pl.when(even)
    def _():
        for q in range(GROUPS):
            fwd(q).wait_send()

    @pl.when(p < T - 1)
    def _():
        for c in range(NC):
            shift(c, w).wait_send()

    @pl.when(late)
    def _():
        for side in range(sides):
            depth_halo(side).wait_send()
            for c in range(NC):
                relay(c, side).wait_send()

    for stage in range(2):
        for side in range(2):
            edge_copy(stage, side).wait_send()
    for yo in range(SP):
        flat = pb * SP + yo

        @pl.when(jnp.logical_and(lax.rem(flat, stride) == 0, yo != y))
        def _():
            dep_copy(yo).wait_send()

            @pl.when(block == 0)
            def _():
                ini_copy(yo).wait_send()

    @pl.when(is_owner)
    def _():
        whole(b.at[:, :, pl.ds(0, (K - 1) * W)], a2a_s.at[0])
        whole(halo_src.at[:, :, pl.ds(0, (K - 1) * LANES)], a2a_s.at[1])
        whole(eo.at[pl.ds(0, TG * SP - 1)], ret_s)

        @pl.when(block < NG - 1)
        def _():
            for copy in carry():
                copy.wait_send()

        for t in range(0, TG, 2):
            for yo in range(SP):
                sent = jnp.logical_not(jnp.logical_and(t == pb, y == yo))
                if t == 0:
                    sent = jnp.logical_and(sent, block > 0)

                @pl.when(sent)
                def _():
                    pltpu.make_async_copy(cin.at[yo], cin.at[yo], beg_s.at[t * SP + yo]).wait()

    @pl.when(jnp.logical_not(is_owner))
    def _():
        whole(b, a2a_s.at[0])
        whole(halo_src, a2a_s.at[1])


def solution(mesh):
    T, SP = mesh.shape["tm"], mesh.shape["space"]

    def per_device(fine_nodes, init_state, mean_depth):
        RL, NX = mean_depth.shape
        NG = 2 if T % 4 == 0 else 1
        members = T // NG * SP
        W = max(LANES, NX // members)
        K = NX // W
        NC = CHUNKS if K % CHUNKS == 0 else 1
        stride = members // K
        hw = 8
        while hw < T:
            hw *= 2
        per = LANES // (2 * hw)
        nh = -(-3 // per)
        cfg = (T, SP, RL, NX, W, K, stride, hw, per, nh, NG, NC)
        f32, dma = jnp.float32, pltpu.SemaphoreType.DMA
        state = pltpu.VMEM((3, RL, NX), f32)
        R = RL * SP
        sides = 1 if SP == 2 else 2
        edges = pltpu.VMEM((2, 2, 3, 1, NX), f32)
        vmem = pl.BlockSpec(memory_space=pltpu.VMEM)
        return pl.pallas_call(
            functools.partial(kernel, cfg),
            out_shape=pltpu.VMEM(fine_nodes.shape, f32),
            in_specs=[pl.BlockSpec(memory_space=pl.ANY)] * 3,
            out_specs=vmem,
            scratch_shapes=[
                pltpu.VMEM((3, 3, RL, NX), f32), state, pltpu.VMEM((RL, NX), f32),
                state, state, state, state, state, state,
                pltpu.VMEM((nh, RL, K * LANES), f32),
                pltpu.VMEM((3, SUB, NX), f32),
                pltpu.VMEM((sides, 3, SUB, NX), f32),
                pltpu.VMEM((SUB, NX), f32),
                pltpu.VMEM((sides, SUB, NX), f32),
                pltpu.VMEM((SP, RL, W + LANES), f32),
                pltpu.VMEM((R, W + LANES), f32),
                pltpu.VMEM((SP, 3, RL, W + LANES), f32),
                pltpu.VMEM((3, R, W + LANES), f32),
                pltpu.VMEM((T // NG, 3, R, W), f32),
                pltpu.VMEM((T // NG, nh, R, LANES), f32),
                pltpu.VMEM((members, 3, RL, W), f32),
                state, state,
                edges, edges,
                pltpu.VMEM((members, 2, 3, 1, W), f32),
                pltpu.VMEM((2, 3, 1, NX), f32),
                pltpu.VMEM((SP, 3, RL, W), f32),
                pltpu.VMEM((nh, R, LANES), f32),
                pltpu.VMEM((nh, R, LANES), f32),
                pltpu.VMEM((3, R, W + LANES), f32),
                dma((NC,)), dma((NC,)), dma((sides, NC)), dma((sides, NC)), dma((sides,)), dma((sides,)),
                dma((2, 2)), dma((2, 2)), dma((SP,)), dma, dma((SP,)), dma, dma((2,)), dma((2, T // NG)),
                dma, dma((GROUPS,)), dma((GROUPS,)), dma((GROUPS,)),
                dma((2,)), dma((2,)), dma((members,)), dma((GROUPS,)), dma((5,)),
            ],
            compiler_params=pltpu.CompilerParams(
                collective_id=0, has_side_effects=True, vmem_limit_bytes=60 * 1024 * 1024
            ),
        )(fine_nodes, init_state, mean_depth)

    return jax.shard_map(
        per_device,
        mesh=mesh,
        in_specs=(P("tm", None, None, "space", None), P(None, "space", None), P("space", None)),
        out_specs=P("tm", None, None, "space", None),
        check_vma=False,
    )
```

time: 64.2 us -> 53.9 us (0.84); the launches traced: 64.1 us -> 53 us
  Pallas kernels: 62.6 us -> 51.6 us
    pallas_call x1, Pallas kernels: 62.6 us -> 51.6 us  [per_device(): pl.pallas_call(functools.partial(kernel, cfg), out_shape=pltpu.VMEM(fine_...]
where the time goes in v2:
time: 53.9 us; the launch traced here: 53 us
  Pallas kernels  51.6 us (96%)
  local copies, waits for them, and re-layouts  1.41 us (3%)
    pallas_call x1, Pallas kernels, per_device(): pl.pallas_call(functools.partial(kernel, cfg), out_shape=pltpu.VMEM(fine_...  51.6 us
    unnamed x1, local copies, waits for them, and re-layouts  1.41 us

profile of v2, /device:TPU:27, one launch (start us, length us, event | category | flops | bytes accessed | tf_op | source)
XLA Modules:
  0.0 53.0 jit_solution(13857959966115046849)
XLA Ops:
  0.0 51.6 %shard_map.37 = f32[1,3,3,16,4096]{4,3,2,1,0:T(8,128)S(1)} custom-call(f32[1,3,3,16,4096]{4,3,2,1,0:T(8,128)} %u_hbm.1, f32[3,16,4096]{2,1,0:T(8,128)} %init_hbm.1, f32[16,4096]{1,0:T(8,128)} %depth_hbm.1), custom_call_target="tpu_custom_call" | custom-call | tf_op jit(solution)/shard_map/pallas_call | solution.py:651
  51.6 1.4 %copy.5 = f32[1,3,3,16,4096]{4,3,2,1,0:T(8,128)} copy(f32[1,3,3,16,4096]{4,3,2,1,0:T(8,128)S(1)} %shard_map.37) | data formatting | bytes 4718592

commit v3 on v2

--- a/solution.py
+++ b/solution.py
@@ -16,8 +16,10 @@
 TURN = DT * FC
 LANES = 128
 SUB = 8
+DEEP = 2
 CHUNKS = 4
 GROUPS = 4
+PARTS = 8
 
 
 def shift_left(v):
@@ -63,7 +65,7 @@
     w, s0, g, s1, mid, b, halo_src, rsrc, rdst, dhsrc, dhdst, dsrc, dep, isrc, ini, main, halo, cs, ce, cb,
     esrc, edst, eo, redge, cin, chalo, chalo_src, state,
     shift_s, shift_r, rel_s, rel_r, dh_s, dh_r, edge_s, edge_r, dep_s, dep_r, ini_s, ini_r, a2a_s, a2a_r, ret_s, ret_r,
-    fwd_s, fwd_r, c_s, c_r, beg_s, beg_r, in_s,
+    fwd_s, fwd_r, c_s, c_r, beg_s, beg_r, in_s, go_carry, go_shift,
 ):
     T, SP, RL, NX, W, K, stride, hw, per, nh, NG, NC = cfg
     TG = T // NG
@@ -71,8 +73,6 @@
     tpc = K // NC
     sides = 1 if SP == 2 else 2
     p, y = lax.axis_index("tm"), lax.axis_index("space")
-    me = p * SP + y
-    total = T * SP
     block = p // TG
     pb = p - block * TG
     local = pb * SP + y
@@ -97,9 +97,26 @@
 
     barrier = pltpu.get_barrier_semaphore()
 
-    @pl.loop(1, total)
+    members = TG * SP
+    has_next, has_last = block < NG - 1, block > 0
+    crosses = jnp.logical_and(has_next, pb == TG - 1)
+
+    def announce(sem, pp):
+        pl.semaphore_signal(sem, inc=1, device_id=(pp, y), device_id_type=MESH)
+
+    @pl.loop(1, members)
     def _(i):
-        pl.semaphore_signal(barrier, inc=1, device_id=where(lax.rem(me + i, total)), device_id_type=MESH)
+        pl.semaphore_signal(
+            barrier, inc=1, device_id=where(block * members + lax.rem(local + i, members)), device_id_type=MESH
+        )
+
+    @pl.when(has_next)
+    def _():
+        announce(barrier, lax.rem(p + TG, T))
+
+    @pl.when(crosses)
+    def _():
+        announce(barrier, lax.rem(p + 1, T))
 
     loads = [pltpu.make_async_copy(u_hbm.at[0, i], u_ref.at[i], in_s.at[i]) for i in (2, 0, 1)]
     loads.append(pltpu.make_async_copy(depth_hbm, depth_ref, in_s.at[3]))
@@ -107,7 +124,16 @@
     for copy in loads:
         copy.start()
     loads[0].wait()
-    pl.semaphore_wait(barrier, total - 1)
+    first_of_block = jnp.logical_and(has_last, pb == 0)
+    pl.semaphore_wait(barrier, members - 1 + has_last.astype(jnp.int32) + first_of_block.astype(jnp.int32))
+
+    @pl.when(has_last)
+    def _():
+        announce(go_carry, lax.rem(p + T - TG, T))
+
+    @pl.when(first_of_block)
+    def _():
+        announce(go_shift, lax.rem(p + T - 1, T))
 
     def chunk(c):
         return pl.ds(c * WC, WC)
@@ -119,7 +145,7 @@
             device_id=(lax.rem(p + 1, T), y), device_id_type=MESH,
         )
 
-    @pl.when(jnp.logical_and(odd, p < T - 1))
+    @pl.when(jnp.logical_and(odd, pb < TG - 1))
     def _():
         for c in range(NC):
             shift(c, w).start()
@@ -135,17 +161,28 @@
     depth_ref[...] = HALF * depth_ref[...]
 
     lane_h = lax.broadcasted_iota(jnp.int32, (RL, LANES), 1)
-    row8 = lax.broadcasted_iota(jnp.int32, (SUB, NX), 0)
-    row8c = lax.broadcasted_iota(jnp.int32, (SUB, WC), 0)
-
-    def margin(ref, c):
-        after = ref[:, pl.ds((c + 1) % NC * WC, LANES)]
-        before = ref[:, pl.ds((c * WC - LANES) % NX, LANES)]
+
+    def outer_rows(own):
+        sub = lax.broadcasted_iota(jnp.int32, (SUB, own.shape[1]), 0)
+        return jnp.where(sub < DEEP, own[:SUB], pltpu.roll(own[RL - SUB :], SUB - 2 * DEEP, 0))[: 2 * DEEP]
+
+    def outer_tile(parts):
+        if sides == 1:
+            both = parts[0]
+        else:
+            sub = lax.broadcasted_iota(jnp.int32, parts[0].shape, 0)
+            both = jnp.where(sub < DEEP, parts[0], parts[1])
+        return jnp.concatenate([both] * (SUB // (2 * DEEP)), axis=0)
+
+
+    def margin(ref, c, size):
+        after = ref[:, pl.ds((c + 1) * size % NX, LANES)]
+        before = ref[:, pl.ds((c * size - LANES) % NX, LANES)]
         lanes = lax.broadcasted_iota(jnp.int32, after.shape, 1)
         return jnp.where(lanes < LANES // 2, after, before)
 
-    def window(ref, c):
-        return jnp.concatenate([ref[:, chunk(c)], margin(ref, c)], axis=1)
+    def window(ref, c, size=WC):
+        return jnp.concatenate([ref[:, pl.ds(c * size, size)], margin(ref, c, size)], axis=1)
 
     def depth_halo(side):
         return pltpu.make_async_remote_copy(
@@ -155,7 +192,7 @@
 
     @pl.when(late)
     def _():
-        dhsrc[...] = jnp.where(row8 < SUB // 2, depth_ref[:SUB], depth_ref[RL - SUB :])
+        dhsrc[...] = outer_rows(depth_ref[...])
         for side in range(sides):
             depth_halo(side).start()
         s0[...] = jnp.zeros_like(s0)
@@ -215,7 +252,7 @@
             for c in chunks:
                 shift(c, w).wait_recv()
                 for f in range(3):
-                    rsrc[f, :, chunk(c)] = jnp.where(row8c < SUB // 2, w[f, :SUB, chunk(c)], w[f, RL - SUB :, chunk(c)])
+                    rsrc[f, :, chunk(c)] = outer_rows(w[f, :, chunk(c)])
                 for side in range(sides):
                     relay(c, side).start()
 
@@ -295,7 +332,16 @@
             - (1.0 / 24.0) * u_ref[0, f] - (1.0 / 6.0) * u_ref[1, f] + (5.0 / 24.0) * u_ref[2, f]
         )
     send_edges(1, lambda r: [g[f, r : r + 1] for f in range(3)])
-    rates = rate_of_g(1, lambda: relay_chunks(range(NC // 4, NC)))
+    def between_one():
+        @pl.when(crosses)
+        def _():
+            pl.semaphore_wait(go_shift, 1)
+            for c in range(NC):
+                shift(c, w).start()
+
+        relay_chunks(range(NC // 4, NC))
+
+    rates = rate_of_g(1, between_one)
     for f in range(3):
         s2 = s1[f] + rates[f]
         b[f] = (1.0 / 6.0) * s2 + (2.0 / 3.0) * s1[f] - (5.0 / 6.0) * s0[f]
@@ -325,15 +371,8 @@
         return jnp.concatenate([own, tile], axis=0)
 
     def late_chunk(c):
-        if sides == 1:
-            tiles = [window(rdst.at[0, f], c) for f in range(3)]
-            depth_tile = window(dhdst.at[0], c)
-        else:
-            rows8 = lax.broadcasted_iota(jnp.int32, (SUB, WC + LANES), 0)
-            tiles = [
-                jnp.where(rows8 < SUB // 2, window(rdst.at[0, f], c), window(rdst.at[1, f], c)) for f in range(3)
-            ]
-            depth_tile = jnp.where(rows8 < SUB // 2, window(dhdst.at[0], c), window(dhdst.at[1], c))
+        tiles = [outer_tile([window(rdst.at[side, f], c) for side in range(sides)]) for f in range(3)]
+        depth_tile = outer_tile([window(dhdst.at[side], c) for side in range(sides)])
         depth = extended(window(depth_ref, c), depth_tile)
         start = [extended(window(w.at[f], c), tiles[f]) for f in range(3)]
         once = periodic_rate(start, depth)
@@ -505,6 +544,7 @@
                         z = pltpu.roll(z, 2 * hw * (f % per), 1)
                     packed = jnp.where(slots == f % per, z, packed)
                 chalo_src[i] = packed
+            pl.semaphore_wait(go_carry, 1)
             for copy in carry():
                 copy.start()
 
@@ -512,10 +552,10 @@
             def _(t):
                 give(t)
 
-    width = NX // GROUPS
+    width, part = NX // GROUPS, NX // PARTS
 
     def fwd(q):
-        cols = pl.ds(q * width, width)
+        cols = pl.ds(q * part, part)
         return pltpu.make_async_remote_copy(
             src_ref=ce.at[:, :, cols], dst_ref=cb.at[:, :, cols],
             send_sem=fwd_s.at[q], recv_sem=fwd_r.at[q], device_id=(lax.rem(p + 1, T), y), device_id_type=MESH,
@@ -533,44 +573,47 @@
         for q in range(GROUPS):
             whole(cb.at[:, :, pl.ds(q * width, width)], beg_r.at[q])
 
-    rowc = lax.broadcasted_iota(jnp.int32, (RL, WC), 0)
-
-    def finish(q):
-        cols = chunk(q)
-        v = [window(cb.at[f], q) + window(b.at[f], q) for f in range(3)]
-        rates = column_terms(*v, window(depth_ref, q))
-        ups, downs = row_terms(*(v[f][:, :WC] for f in range(3)), depth_ref[:, cols])
+    row_part = lax.broadcasted_iota(jnp.int32, (RL, part), 0)
+
+    def advance(q):
+        cols = pl.ds(q * part, part)
+        v = [window(cb.at[f], q, part) + window(b.at[f], q, part) for f in range(3)]
+        rates = column_terms(*v, window(depth_ref, q, part))
+        ups, downs = row_terms(*(v[f][:, :part] for f in range(3)), depth_ref[:, cols])
+        return [
+            cb[f, :, cols] + rates[f][:, :part]
+            + jnp.where(row_part == RL - 1, redge[0, f, :, cols], shift_up(ups[f]))
+            + jnp.where(row_part == 0, redge[1, f, :, cols], shift_down(downs[f]))
+            for f in range(3)
+        ]
+
+    def emit(q, ends):
+        cols = pl.ds(q * part, part)
         for f in range(3):
             start = cb[f, :, cols]
-            end = (
-                start + rates[f][:, :WC]
-                + jnp.where(rowc == RL - 1, redge[0, f, :, cols], shift_up(ups[f]))
-                + jnp.where(rowc == 0, redge[1, f, :, cols], shift_down(downs[f]))
-            )
-            ce[f, :, cols] = end
             out_ref[0, 0, f, :, cols] = start
-            out_ref[0, 1, f, :, cols] = mid[f, :, cols] + 0.5 * (start + end)
-            out_ref[0, 2, f, :, cols] = end
+            out_ref[0, 1, f, :, cols] = mid[f, :, cols] + 0.5 * (start + ends[f])
+            out_ref[0, 2, f, :, cols] = ends[f]
 
     @pl.when(even)
     def _():
-        for q in range(NC):
-            finish(q)
+        for q in range(PARTS):
+            ends = advance(q)
+            for f in range(3):
+                ce[f, :, pl.ds(q * part, part)] = ends[f]
             fwd(q).start()
+        for q in range(PARTS):
+            emit(q, [ce[f, :, pl.ds(q * part, part)] for f in range(3)])
+            fwd(q).wait_send()
 
     @pl.when(odd)
     def _():
         arrived = 0
-        for step in range(1, NC + 1):
-            while arrived < min(step + 2, NC):
+        for step in range(1, PARTS + 1):
+            while arrived < min(step + 2, PARTS):
                 fwd(arrived).wait_recv()
                 arrived += 1
-            finish(step % NC)
-
-    @pl.when(even)
-    def _():
-        for q in range(GROUPS):
-            fwd(q).wait_send()
+            emit(step % PARTS, advance(step % PARTS))
 
     @pl.when(p < T - 1)
     def _():
@@ -657,10 +700,10 @@
                 pltpu.VMEM((3, 3, RL, NX), f32), state, pltpu.VMEM((RL, NX), f32),
                 state, state, state, state, state, state,
                 pltpu.VMEM((nh, RL, K * LANES), f32),
-                pltpu.VMEM((3, SUB, NX), f32),
-                pltpu.VMEM((sides, 3, SUB, NX), f32),
-                pltpu.VMEM((SUB, NX), f32),
-                pltpu.VMEM((sides, SUB, NX), f32),
+                pltpu.VMEM((3, 2 * DEEP, NX), f32),
+                pltpu.VMEM((sides, 3, 2 * DEEP, NX), f32),
+                pltpu.VMEM((2 * DEEP, NX), f32),
+                pltpu.VMEM((sides, 2 * DEEP, NX), f32),
                 pltpu.VMEM((SP, RL, W + LANES), f32),
                 pltpu.VMEM((R, W + LANES), f32),
                 pltpu.VMEM((SP, 3, RL, W + LANES), f32),
@@ -678,8 +721,9 @@
                 pltpu.VMEM((3, R, W + LANES), f32),
                 dma((NC,)), dma((NC,)), dma((sides, NC)), dma((sides, NC)), dma((sides,)), dma((sides,)),
                 dma((2, 2)), dma((2, 2)), dma((SP,)), dma, dma((SP,)), dma, dma((2,)), dma((2, T // NG)),
-                dma, dma((GROUPS,)), dma((GROUPS,)), dma((GROUPS,)),
+                dma, dma((GROUPS,)), dma((PARTS,)), dma((PARTS,)),
                 dma((2,)), dma((2,)), dma((members,)), dma((GROUPS,)), dma((5,)),
+                pltpu.SemaphoreType.REGULAR, pltpu.SemaphoreType.REGULAR,
             ],
             compiler_params=pltpu.CompilerParams(
                 collective_id=0, has_side_effects=True, vmem_limit_bytes=60 * 1024 * 1024

time: 53.9 us -> 48.9 us (0.907)
  Pallas kernels: 51.6 us -> 46.7 us
    pallas_call x1, Pallas kernels: 51.6 us -> 46.7 us  [per_device(): pl.pallas_call(functools.partial(kernel, cfg), out_shape=pltpu.VMEM(fine_...]
where the time goes in v3:
time: 48.9 us; the launch traced here: 48.1 us
  Pallas kernels  46.7 us (96%)
  local copies, waits for them, and re-layouts  1.41 us (3%)
    pallas_call x1, Pallas kernels, per_device(): pl.pallas_call(functools.partial(kernel, cfg), out_shape=pltpu.VMEM(fine_...  46.7 us
    unnamed x1, local copies, waits for them, and re-layouts  1.41 us

profile of v3, /device:TPU:27, one launch (start us, length us, event | category | flops | bytes accessed | tf_op | source)
XLA Modules:
  0.0 48.1 jit_solution(434816203465908307)
XLA Ops:
  0.0 46.7 %shard_map.37 = f32[1,3,3,16,4096]{4,3,2,1,0:T(8,128)S(1)} custom-call(f32[1,3,3,16,4096]{4,3,2,1,0:T(8,128)} %u_hbm.1, f32[3,16,4096]{2,1,0:T(8,128)} %init_hbm.1, f32[16,4096]{1,0:T(8,128)} %depth_hbm.1), custom_call_target="tpu_custom_call" | custom-call | tf_op jit(solution)/shard_map/pallas_call | solution.py:694
  46.7 1.4 %copy.5 = f32[1,3,3,16,4096]{4,3,2,1,0:T(8,128)} copy(f32[1,3,3,16,4096]{4,3,2,1,0:T(8,128)S(1)} %shard_map.37) | data formatting | bytes 4718592

commit v4 on v3

--- a/solution.py
+++ b/solution.py
@@ -20,6 +20,7 @@
 CHUNKS = 4
 GROUPS = 4
 PARTS = 8
+SPANS = 2
 
 
 def shift_left(v):
@@ -60,12 +61,46 @@
     return [rates[f] + shift_up(ups[f]) + shift_down(downs[f]) for f in range(3)]
 
 
+class Tile:
+    def __init__(self, state, depth):
+        h, e, n = state
+        de, dn = depth * e, depth * n
+        nh, ne, nn, hh = DIFF * h, DIFF * e, DIFF * n, HALF * h
+        self.lefts = [shift_left(x) for x in (nh - de, ne - hh, nn)]
+        self.rights = [shift_right(x) for x in (nh + de, ne + hh, nn)]
+        self.ups, self.downs = (nh - dn, ne, nn - hh), (nh + dn, ne, nn + hh)
+        self.own = (-4.0 * nh, TURN * n - 4.0 * ne, -4.0 * nn - TURN * e)
+
+
+def column_sum(before, tile, after, f, lane):
+    return (
+        tile.own[f]
+        + jnp.where(lane == LANES - 1, after.lefts[f], tile.lefts[f])
+        + jnp.where(lane == 0, before.rights[f], tile.rights[f])
+    )
+
+
+def walk(load, tiles, count, visit, made=None):
+    made = {} if made is None else made
+
+    def tile(i):
+        i %= count
+        if i not in made:
+            made[i] = Tile(*load(i))
+        return made[i]
+
+    for j in tiles:
+        visit(j, tile(j - 1), tile(j), tile(j + 1))
+        if count > 4:
+            made.pop((j - 1) % count)
+
+
 def kernel(
     cfg, u_hbm, init_hbm, depth_hbm, out_ref, u_ref, init_ref, depth_ref,
     w, s0, g, s1, mid, b, halo_src, rsrc, rdst, dhsrc, dhdst, dsrc, dep, isrc, ini, main, halo, cs, ce, cb,
     esrc, edst, eo, redge, cin, chalo, chalo_src, state,
     shift_s, shift_r, rel_s, rel_r, dh_s, dh_r, edge_s, edge_r, dep_s, dep_r, ini_s, ini_r, a2a_s, a2a_r, ret_s, ret_r,
-    fwd_s, fwd_r, c_s, c_r, beg_s, beg_r, in_s, go_carry, go_shift,
+    fwd_s, fwd_r, c_s, c_r, beg_s, beg_r, in_s, go_carry,
 ):
     T, SP, RL, NX, W, K, stride, hw, per, nh, NG, NC = cfg
     TG = T // NG
@@ -125,15 +160,17 @@
         copy.start()
     loads[0].wait()
     first_of_block = jnp.logical_and(has_last, pb == 0)
-    pl.semaphore_wait(barrier, members - 1 + has_last.astype(jnp.int32) + first_of_block.astype(jnp.int32))
+    meets = jnp.logical_or(crosses, first_of_block)
+
+    @pl.when(first_of_block)
+    def _():
+        announce(barrier, lax.rem(p + T - 1, T))
+
+    pl.semaphore_wait(barrier, members - 1 + has_last.astype(jnp.int32) + meets.astype(jnp.int32))
 
     @pl.when(has_last)
     def _():
         announce(go_carry, lax.rem(p + T - TG, T))
-
-    @pl.when(first_of_block)
-    def _():
-        announce(go_shift, lax.rem(p + T - 1, T))
 
     def chunk(c):
         return pl.ds(c * WC, WC)
@@ -145,7 +182,7 @@
             device_id=(lax.rem(p + 1, T), y), device_id_type=MESH,
         )
 
-    @pl.when(jnp.logical_and(odd, pb < TG - 1))
+    @pl.when(jnp.logical_and(odd, p < T - 1))
     def _():
         for c in range(NC):
             shift(c, w).start()
@@ -206,38 +243,52 @@
         for c in range(NC):
             shift(c, s0).wait_recv()
 
-    row = lax.broadcasted_iota(jnp.int32, (RL, NX), 0)
-
-    def edge_copy(stage, side):
+    row = lax.broadcasted_iota(jnp.int32, (RL, LANES), 0)
+    lane = lax.broadcasted_iota(jnp.int32, (RL, LANES), 1)
+    NT = NX // LANES
+    SPAN = NX // SPANS
+
+    def lanes_of(j):
+        return slice(j * LANES, (j + 1) * LANES)
+
+    def edge_copy(stage, side, part):
+        cols = pl.ds(part * SPAN, SPAN)
         return pltpu.make_async_remote_copy(
-            src_ref=esrc.at[stage, side], dst_ref=edst.at[stage, side],
-            send_sem=edge_s.at[stage, side], recv_sem=edge_r.at[stage, side],
+            src_ref=esrc.at[stage, side, :, :, cols], dst_ref=edst.at[stage, side, :, :, cols],
+            send_sem=edge_s.at[stage, side, part], recv_sem=edge_r.at[stage, side, part],
             device_id=(p, row_neighbour(side)), device_id_type=MESH,
         )
 
-    def send_edges(stage, rows_of):
-        top, bottom = rows_of(0), rows_of(RL - 1)
-        up0, _ = row_terms(*top, depth_ref[0:1])
-        _, down1 = row_terms(*bottom, depth_ref[RL - 1 : RL])
+    def put_edges(stage, cols, top, bottom):
+        ups, _ = row_terms(*top, depth_ref[0:1, cols])
+        _, downs = row_terms(*bottom, depth_ref[RL - 1 : RL, cols])
         for f in range(3):
-            esrc[stage, 0, f] = up0[f]
-            esrc[stage, 1, f] = down1[f]
+            esrc[stage, 0, f, :, cols] = ups[f]
+            esrc[stage, 1, f, :, cols] = downs[f]
+
+    def send_edges(stage, part):
         for side in range(2):
-            edge_copy(stage, side).start()
-
-    def rate_of_g(stage, between):
-        between()
-        h, e, n, depth = g[0], g[1], g[2], depth_ref[...]
-        rates = column_terms(h, e, n, depth)
-        ups, downs = row_terms(h, e, n, depth)
+            edge_copy(stage, side, part).start()
+
+    def wait_edges(stage, part):
         for side in range(2):
-            edge_copy(stage, side).wait_recv()
-        return [
-            rates[f]
-            + jnp.where(row == RL - 1, edst[stage, 0, f], shift_up(ups[f]))
-            + jnp.where(row == 0, edst[stage, 1, f], shift_down(downs[f]))
-            for f in range(3)
-        ]
+            edge_copy(stage, side, part).wait_recv()
+
+    def inner_rate(load, out):
+        def visit(j, before, tile, after):
+            for f in range(3):
+                out[f, :, lanes_of(j)] = (
+                    column_sum(before, tile, after, f, lane)
+                    + jnp.where(row == RL - 1, 0.0, shift_up(tile.ups[f]))
+                    + jnp.where(row == 0, 0.0, shift_down(tile.downs[f]))
+                )
+
+        walk(load, range(NT), NT, visit)
+
+    def outer_rate(stage, f, cols):
+        return jnp.where(
+            row == RL - 1, edst[stage, 0, f, :, cols], jnp.where(row == 0, edst[stage, 1, f, :, cols], 0.0)
+        )
 
     def relay(c, side):
         return pltpu.make_async_remote_copy(
@@ -256,15 +307,20 @@
                 for side in range(sides):
                     relay(c, side).start()
 
-    def first_g(rows, f):
+    def first_g(rows, cols, f):
         return (
-            (-7.0 / 24.0) * u_ref[0, f, rows] + (1.0 / 3.0) * u_ref[1, f, rows] - (1.0 / 24.0) * u_ref[2, f, rows]
-            + 0.5 * s0[f, rows]
-        )
-
-    send_edges(0, lambda r: [first_g(slice(r, r + 1), f) for f in range(3)])
-    for f in range(3):
-        g[f] = first_g(slice(0, RL), f)
+            (-7.0 / 24.0) * u_ref[0, f, rows, cols] + (1.0 / 3.0) * u_ref[1, f, rows, cols]
+            - (1.0 / 24.0) * u_ref[2, f, rows, cols] + 0.5 * s0[f, rows, cols]
+        )
+
+    every = slice(0, RL)
+    for part in range(SPANS):
+        for j in range(part * SPAN // LANES, (part + 1) * SPAN // LANES):
+            put_edges(0, lanes_of(j), *([first_g(slice(r, r + 1), lanes_of(j), f) for f in range(3)] for r in (0, RL - 1)))
+        send_edges(0, part)
+    inner_rate(
+        lambda j: ([first_g(every, lanes_of(j), f) for f in range(3)], depth_ref[:, lanes_of(j)]), s1
+    )
 
     def dep_copy(yo):
         return pltpu.make_async_remote_copy(
@@ -319,33 +375,25 @@
                         isrc.at[yo], ini.at[:, pl.ds(pl.multiple_of(y * RL, 8), RL)], ini_r
                     ).start()
 
-    def between_zero():
-        owner_tables()
-        relay_chunks(range(0, NC // 4))
-
-    rates = rate_of_g(0, between_zero)
-    for f in range(3):
-        s1[f] = s0[f] + rates[f]
-    for f in range(3):
-        g[f] = (
-            0.5 * s1[f]
-            - (1.0 / 24.0) * u_ref[0, f] - (1.0 / 6.0) * u_ref[1, f] + (5.0 / 24.0) * u_ref[2, f]
-        )
-    send_edges(1, lambda r: [g[f, r : r + 1] for f in range(3)])
-    def between_one():
-        @pl.when(crosses)
-        def _():
-            pl.semaphore_wait(go_shift, 1)
-            for c in range(NC):
-                shift(c, w).start()
-
-        relay_chunks(range(NC // 4, NC))
-
-    rates = rate_of_g(1, between_one)
-    for f in range(3):
-        s2 = s1[f] + rates[f]
-        b[f] = (1.0 / 6.0) * s2 + (2.0 / 3.0) * s1[f] - (5.0 / 6.0) * s0[f]
-        mid[f] = s1[f] - 0.5 * (s0[f] + s2)
+    owner_tables()
+    for part in range(SPANS):
+        wait_edges(0, part)
+        for j in range(part * SPAN // LANES, (part + 1) * SPAN // LANES):
+            cols = lanes_of(j)
+            new = []
+            for f in range(3):
+                one = s0[f, :, cols] + s1[f, :, cols] + outer_rate(0, f, cols)
+                s1[f, :, cols] = one
+                new.append(
+                    0.5 * one - (1.0 / 24.0) * u_ref[0, f, :, cols] - (1.0 / 6.0) * u_ref[1, f, :, cols]
+                    + (5.0 / 24.0) * u_ref[2, f, :, cols]
+                )
+                g[f, :, cols] = new[f]
+            put_edges(1, cols, [v[0:1] for v in new], [v[RL - 1 : RL] for v in new])
+        send_edges(1, part)
+    inner_rate(lambda j: ([g[f, :, lanes_of(j)] for f in range(3)], depth_ref[:, lanes_of(j)]), b)
+
+    relay_chunks(range(NC))
 
     my_rows = pl.ds(pl.multiple_of(y * RL, 8), RL)
 
@@ -366,6 +414,36 @@
         @pl.when(j * stride == local)
         def _():
             pltpu.make_async_copy(src, dst, a2a_r.at[i, pb]).start()
+
+    for part in range(SPANS):
+        wait_edges(1, part)
+        for j in range(part * SPAN // LANES, (part + 1) * SPAN // LANES):
+            cols = lanes_of(j)
+            for f in range(3):
+                start, one = s0[f, :, cols], s1[f, :, cols]
+                two = one + b[f, :, cols] + outer_rate(1, f, cols)
+                b[f, :, cols] = (1.0 / 6.0) * two + (2.0 / 3.0) * one - (5.0 / 6.0) * start
+                mid[f, :, cols] = one - 0.5 * (start + two)
+
+    slot_of = lax.rem(lane_h + hw, LANES) // (2 * hw)
+
+    def send_halo(k):
+        lo, hi = ((k + 1) % K) * W, (k * W - LANES) % NX
+        packed = [jnp.zeros((RL, LANES), jnp.float32) for _ in range(nh)]
+        for f in range(3):
+            z = jnp.where(lane_h < LANES // 2, b[f, :, lo : lo + LANES], b[f, :, hi : hi + LANES])
+            slot = f % per
+            if slot:
+                z = pltpu.roll(z, 2 * hw * slot, 1)
+            packed[f // per] = jnp.where(slot_of == slot, z, packed[f // per])
+        for i in range(nh):
+            halo_src[i, :, k * LANES : (k + 1) * LANES] = packed[i]
+
+    def send_halos(ks):
+        for k in ks:
+            send_halo(k)
+        for k in ks:
+            a2a(1, k)
 
     def extended(own, tile):
         return jnp.concatenate([own, tile], axis=0)
@@ -390,7 +468,7 @@
     def _():
         for side in range(sides):
             depth_halo(side).wait_recv()
-        arrived = 0
+        arrived, known, sent = 0, set(), set()
         for step in range(1, NC + 1):
             c = step % NC
             while arrived < min(step + 2, NC):
@@ -398,29 +476,20 @@
                     relay(arrived, side).wait_recv()
                 arrived += 1
             late_chunk(c)
+            known.update(range(c * tpc, (c + 1) * tpc))
+            ready = [k for k in range(K) if k not in sent and {(k - 1) % K, k, (k + 1) % K} <= known]
+            sent.update(ready)
+            send_halos(ready)
 
     @pl.when(jnp.logical_not(late))
     def _():
         @pl.loop(0, K)
         def _(i):
-            a2a(0, lax.rem(mine + i, K))
-
-    slot_of = lax.rem(lane_h + hw, LANES) // (2 * hw)
-    for k in range(K):
-        lo, hi = ((k + 1) % K) * W, (k * W - LANES) % NX
-        packed = [jnp.zeros((RL, LANES), jnp.float32) for _ in range(nh)]
-        for f in range(3):
-            z = jnp.where(lane_h < LANES // 2, b[f, :, lo : lo + LANES], b[f, :, hi : hi + LANES])
-            slot = f % per
-            if slot:
-                z = pltpu.roll(z, 2 * hw * slot, 1)
-            packed[f // per] = jnp.where(slot_of == slot, z, packed[f // per])
-        for i in range(nh):
-            halo_src[i, :, k * LANES : (k + 1) * LANES] = packed[i]
-
-    @pl.loop(0, K)
-    def _(i):
-        a2a(1, lax.rem(mine + i, K))
+            c = i // tpc
+            c = lax.rem(c * 2, NC) + lax.rem(y + c * 2 // NC, 2) if NC > 1 else c
+            a2a(0, c * tpc + lax.rem(mine + i, tpc))
+
+        send_halos(range(K))
 
     my_tile = pl.ds(pl.multiple_of(mine * W, LANES), W)
     my_group = mine // (K // GROUPS)
@@ -485,31 +554,39 @@
     @pl.when(is_owner)
     def _():
         whole(dep, dep_r)
-        depth = dep[...]
-
-        def turn(t, cur):
+
+        ring = W // LANES + 1
+        tall = lax.broadcasted_iota(jnp.int32, (R, LANES), 1)
+
+        def turn(t, carried):
             whole(main.at[t], a2a_r.at[0, t])
             whole(halo.at[t], a2a_r.at[1, t])
-            h, e, n = (
-                cur[f] + jnp.concatenate([main[t, f], unpack(halo[t, f // per], f)], axis=1) for f in range(3)
-            )
-            rates = column_terms(h, e, n, depth)
-            ups, downs = row_terms(h, e, n, depth)
-            new = []
-            for f in range(3):
-                value = cur[f] + (rates[f] + shift_up(ups[f]) + shift_down(downs[f]))
-                for yo in range(SP):
-                    cs[t * SP + yo, f] = value[yo * RL : (yo + 1) * RL, :W]
-                    below, above = (yo + 1) * RL % R, (yo * RL - 1) % R
-                    eo[t * SP + yo, 0, f] = ups[f][below : below + 1, :W]
-                    eo[t * SP + yo, 1, f] = downs[f][above : above + 1, :W]
-                new.append(value)
+            cur = [[state[f, :, lanes_of(j)] for f in range(3)] for j in range(ring)]
+
+            def load(j):
+                sent = [main[t, f, :, lanes_of(j)] if j < ring - 1 else unpack(halo[t, f // per], f) for f in range(3)]
+                return [cur[j][f] + sent[f] for f in range(3)], dep[:, lanes_of(j)]
+
+            def visit(j, before, tile, after):
+                for f in range(3):
+                    value = cur[j][f] + (
+                        column_sum(before, tile, after, f, tall) + shift_up(tile.ups[f]) + shift_down(tile.downs[f])
+                    )
+                    state[f, :, lanes_of(j)] = value
+                    if j < ring - 1:
+                        for yo in range(SP):
+                            cs[t * SP + yo, f, :, lanes_of(j)] = value[yo * RL : (yo + 1) * RL]
+                            below, above = (yo + 1) * RL % R, (yo * RL - 1) % R
+                            eo[t * SP + yo, 0, f, :, lanes_of(j)] = tile.ups[f][below : below + 1]
+                            eo[t * SP + yo, 1, f, :, lanes_of(j)] = tile.downs[f][above : above + 1]
+
+            walk(load, range(ring), ring, visit)
 
             @pl.when(jnp.logical_and(t > 0, block == NG - 1))
             def _():
                 give(t - 1)
 
-            return tuple(new)
+            return carried
 
         @pl.when(block == 0)
         def _():
@@ -526,7 +603,7 @@
                     state[f, yo * RL : (yo + 1) * RL, :W] = cin[yo, f]
                 state[f, :, W:] = unpack(chalo[f // per], f)
 
-        last = lax.fori_loop(0, TG, turn, tuple(state[f] for f in range(3)))
+        lax.fori_loop(0, TG, turn, 0)
 
         @pl.when(block == NG - 1)
         def _():
@@ -539,7 +616,7 @@
             for i in range(nh):
                 packed = jnp.zeros((SP * RL, LANES), jnp.float32)
                 for f in range(i * per, min(3, (i + 1) * per)):
-                    z = last[f][:, W:]
+                    z = state[f, :, W:]
                     if f % per:
                         z = pltpu.roll(z, 2 * hw * (f % per), 1)
                     packed = jnp.where(slots == f % per, z, packed)
@@ -573,47 +650,55 @@
         for q in range(GROUPS):
             whole(cb.at[:, :, pl.ds(q * width, width)], beg_r.at[q])
 
-    row_part = lax.broadcasted_iota(jnp.int32, (RL, part), 0)
-
-    def advance(q):
-        cols = pl.ds(q * part, part)
-        v = [window(cb.at[f], q, part) + window(b.at[f], q, part) for f in range(3)]
-        rates = column_terms(*v, window(depth_ref, q, part))
-        ups, downs = row_terms(*(v[f][:, :part] for f in range(3)), depth_ref[:, cols])
-        return [
-            cb[f, :, cols] + rates[f][:, :part]
-            + jnp.where(row_part == RL - 1, redge[0, f, :, cols], shift_up(ups[f]))
-            + jnp.where(row_part == 0, redge[1, f, :, cols], shift_down(downs[f]))
-            for f in range(3)
-        ]
-
-    def emit(q, ends):
-        cols = pl.ds(q * part, part)
+    per_part = NT // PARTS
+
+    def advance(q, made, visit_ends):
+        def load(j):
+            return [cb[f, :, lanes_of(j)] + b[f, :, lanes_of(j)] for f in range(3)], depth_ref[:, lanes_of(j)]
+
+        def visit(j, before, tile, after):
+            cols = lanes_of(j)
+            visit_ends(cols, [
+                cb[f, :, cols] + column_sum(before, tile, after, f, lane)
+                + jnp.where(row == RL - 1, redge[0, f, :, cols], shift_up(tile.ups[f]))
+                + jnp.where(row == 0, redge[1, f, :, cols], shift_down(tile.downs[f]))
+                for f in range(3)
+            ])
+
+        walk(load, range(q * per_part, (q + 1) * per_part), NT, visit, made)
+
+    def keep(cols, ends):
+        for f in range(3):
+            ce[f, :, cols] = ends[f]
+
+    def emit(cols, ends):
         for f in range(3):
             start = cb[f, :, cols]
             out_ref[0, 0, f, :, cols] = start
             out_ref[0, 1, f, :, cols] = mid[f, :, cols] + 0.5 * (start + ends[f])
             out_ref[0, 2, f, :, cols] = ends[f]
 
+    order = [PARTS - 1, *range(PARTS - 1)]
+
     @pl.when(even)
     def _():
+        made = {}
+        for q in order:
+            advance(q, made, keep)
+            fwd(q).start()
+        for j in range(NT):
+            emit(lanes_of(j), [ce[f, :, lanes_of(j)] for f in range(3)])
+        for q in order:
+            fwd(q).wait_send()
+
+    @pl.when(odd)
+    def _():
+        made, arrived = {}, 0
         for q in range(PARTS):
-            ends = advance(q)
-            for f in range(3):
-                ce[f, :, pl.ds(q * part, part)] = ends[f]
-            fwd(q).start()
-        for q in range(PARTS):
-            emit(q, [ce[f, :, pl.ds(q * part, part)] for f in range(3)])
-            fwd(q).wait_send()
-
-    @pl.when(odd)
-    def _():
-        arrived = 0
-        for step in range(1, PARTS + 1):
-            while arrived < min(step + 2, PARTS):
-                fwd(arrived).wait_recv()
+            while arrived < min(q + 3, PARTS):
+                fwd(order[arrived]).wait_recv()
                 arrived += 1
-            emit(step % PARTS, advance(step % PARTS))
+            advance(q, made, emit)
 
     @pl.when(p < T - 1)
     def _():
@@ -629,7 +714,8 @@
 
     for stage in range(2):
         for side in range(2):
-            edge_copy(stage, side).wait_send()
+            for part in range(SPANS):
+                edge_copy(stage, side, part).wait_send()
     for yo in range(SP):
         flat = pb * SP + yo
 
@@ -720,10 +806,10 @@
                 pltpu.VMEM((nh, R, LANES), f32),
                 pltpu.VMEM((3, R, W + LANES), f32),
                 dma((NC,)), dma((NC,)), dma((sides, NC)), dma((sides, NC)), dma((sides,)), dma((sides,)),
-                dma((2, 2)), dma((2, 2)), dma((SP,)), dma, dma((SP,)), dma, dma((2,)), dma((2, T // NG)),
+                dma((2, 2, SPANS)), dma((2, 2, SPANS)), dma((SP,)), dma, dma((SP,)), dma, dma((2,)), dma((2, T // NG)),
                 dma, dma((GROUPS,)), dma((PARTS,)), dma((PARTS,)),
                 dma((2,)), dma((2,)), dma((members,)), dma((GROUPS,)), dma((5,)),
-                pltpu.SemaphoreType.REGULAR, pltpu.SemaphoreType.REGULAR,
+                pltpu.SemaphoreType.REGULAR,
             ],
             compiler_params=pltpu.CompilerParams(
                 collective_id=0, has_side_effects=True, vmem_limit_bytes=60 * 1024 * 1024

time: 48.9 us -> 45.4 us (0.928)
  Pallas kernels: 46.7 us -> 43.6 us
    pallas_call x1, Pallas kernels: 46.7 us -> 43.6 us  [per_device(): pl.pallas_call(functools.partial(kernel, cfg), out_shape=pltpu.VMEM(fine_...]
where the time goes in v4:
time: 45.4 us; the launch traced here: 45 us
  Pallas kernels  43.6 us (96%)
  local copies, waits for them, and re-layouts  1.41 us (3%)
    pallas_call x1, Pallas kernels, per_device(): pl.pallas_call(functools.partial(kernel, cfg), out_shape=pltpu.VMEM(fine_...  43.6 us
    unnamed x1, local copies, waits for them, and re-layouts  1.41 us

profile of v4, /device:TPU:27, one launch (start us, length us, event | category | flops | bytes accessed | tf_op | source)
XLA Modules:
  0.0 45.0 jit_solution(14113715393703097319)
XLA Ops:
  0.0 43.6 %shard_map.37 = f32[1,3,3,16,4096]{4,3,2,1,0:T(8,128)S(1)} custom-call(f32[1,3,3,16,4096]{4,3,2,1,0:T(8,128)} %u_hbm.1, f32[3,16,4096]{2,1,0:T(8,128)} %init_hbm.1, f32[16,4096]{1,0:T(8,128)} %depth_hbm.1), custom_call_target="tpu_custom_call" | custom-call | tf_op jit(solution)/shard_map/pallas_call | solution.py:780
  43.6 1.4 %copy.5 = f32[1,3,3,16,4096]{4,3,2,1,0:T(8,128)} copy(f32[1,3,3,16,4096]{4,3,2,1,0:T(8,128)S(1)} %shard_map.37) | data formatting | bytes 4718592

commit v5 on v4

--- a/solution.py
+++ b/solution.py
@@ -18,9 +18,10 @@
 SUB = 8
 DEEP = 2
 CHUNKS = 4
-GROUPS = 4
+SPREAD = 4
 PARTS = 8
 SPANS = 2
+HOLD = 4
 
 
 def shift_left(v):
@@ -116,11 +117,15 @@
     odd = jnp.logical_not(even)
     late = jnp.logical_and(even, p > 0)
 
+    spread = SPREAD if NC % SPREAD == 0 else 1
+
     def tile_of(j):
-        return lax.rem(j, NC) * tpc + j // NC
+        high, low = j // (tpc * spread), lax.rem(j, spread)
+        return (high * spread + low) * tpc + lax.rem(j // spread, tpc)
 
     def owner_of(k):
-        return lax.rem(k, tpc) * NC + k // tpc
+        c = k // tpc
+        return c // spread * (tpc * spread) + lax.rem(k, tpc) * spread + lax.rem(c, spread)
 
     mine = tile_of(local // stride)
 
@@ -172,13 +177,16 @@
     def _():
         announce(go_carry, lax.rem(p + T - TG, T))
 
+    def whole(ref, sem):
+        pltpu.make_async_copy(ref, ref, sem).wait()
+
     def chunk(c):
         return pl.ds(c * WC, WC)
 
     def shift(c, dst):
         return pltpu.make_async_remote_copy(
             src_ref=u_ref.at[2, :, :, chunk(c)], dst_ref=dst.at[:, :, chunk(c)],
-            send_sem=shift_s.at[c], recv_sem=shift_r.at[c],
+            send_sem=shift_s, recv_sem=shift_r.at[c],
             device_id=(lax.rem(p + 1, T), y), device_id_type=MESH,
         )
 
@@ -255,7 +263,7 @@
         cols = pl.ds(part * SPAN, SPAN)
         return pltpu.make_async_remote_copy(
             src_ref=esrc.at[stage, side, :, :, cols], dst_ref=edst.at[stage, side, :, :, cols],
-            send_sem=edge_s.at[stage, side, part], recv_sem=edge_r.at[stage, side, part],
+            send_sem=edge_s, recv_sem=edge_r.at[stage, part],
             device_id=(p, row_neighbour(side)), device_id_type=MESH,
         )
 
@@ -271,8 +279,7 @@
             edge_copy(stage, side, part).start()
 
     def wait_edges(stage, part):
-        for side in range(2):
-            edge_copy(stage, side, part).wait_recv()
+        whole(edst.at[stage, :, :, :, pl.ds(part * SPAN, SPAN)], edge_r.at[stage, part])
 
     def inner_rate(load, out):
         def visit(j, before, tile, after):
@@ -293,7 +300,7 @@
     def relay(c, side):
         return pltpu.make_async_remote_copy(
             src_ref=rsrc.at[:, :, chunk(c)], dst_ref=rdst.at[side, :, :, chunk(c)],
-            send_sem=rel_s.at[side, c], recv_sem=rel_r.at[side, c],
+            send_sem=rel_s.at[side], recv_sem=rel_r.at[side, c],
             device_id=(p, row_neighbour(side)), device_id_type=MESH,
         )
 
@@ -390,10 +397,21 @@
                 )
                 g[f, :, cols] = new[f]
             put_edges(1, cols, [v[0:1] for v in new], [v[RL - 1 : RL] for v in new])
-        send_edges(1, part)
+
+        @pl.when(jnp.logical_not(late))
+        def _():
+            send_edges(1, part)
+
     inner_rate(lambda j: ([g[f, :, lanes_of(j)] for f in range(3)], depth_ref[:, lanes_of(j)]), b)
 
-    relay_chunks(range(NC))
+    relay_chunks(range(HOLD * NC // 8))
+
+    @pl.when(late)
+    def _():
+        for part in range(SPANS):
+            send_edges(1, part)
+
+    relay_chunks(range(HOLD * NC // 8, NC))
 
     my_rows = pl.ds(pl.multiple_of(y * RL, 8), RL)
 
@@ -491,155 +509,161 @@
 
         send_halos(range(K))
 
-    my_tile = pl.ds(pl.multiple_of(mine * W, LANES), W)
-    my_group = mine // (K // GROUPS)
-
-    def give_edges(t):
+    NS = W // LANES
+
+    def my_lanes(i):
+        return pl.ds(pl.multiple_of(mine * W + i * LANES, LANES), LANES)
+
+    def hand(src, dst, send, recv, t, yo):
+        here = jnp.logical_and(t == pb, y == yo)
+
+        @pl.when(jnp.logical_not(here))
+        def _():
+            pltpu.make_async_remote_copy(
+                src_ref=src, dst_ref=dst, send_sem=send, recv_sem=recv,
+                device_id=(block * TG + t, yo), device_id_type=MESH,
+            ).start()
+
+        @pl.when(here)
+        def _():
+            pltpu.make_async_copy(src, dst, recv).start()
+
+    def give_begin(i, t, src):
         for yo in range(SP):
-            src, dst = eo.at[t * SP + yo], redge.at[:, :, :, my_tile]
-            here = jnp.logical_and(t == pb, y == yo)
-
-            @pl.when(jnp.logical_not(here))
-            def _():
-                pltpu.make_async_remote_copy(
-                    src_ref=src, dst_ref=dst, send_sem=ret_s, recv_sem=ret_r.at[my_group],
-                    device_id=(block * TG + t, yo), device_id_type=MESH,
-                ).start()
-
-            @pl.when(here)
-            def _():
-                pltpu.make_async_copy(src, dst, ret_r.at[my_group]).start()
-
-    def give_begin(t, src):
+            hand(src.at[yo], cb.at[:, :, my_lanes(i)], beg_s, beg_r, t, yo)
+
+    def give(i, t):
         for yo in range(SP):
-            dst = cb.at[:, :, my_tile]
-            here = jnp.logical_and(t == pb, y == yo)
-
-            @pl.when(jnp.logical_not(here))
-            def _():
-                pltpu.make_async_remote_copy(
-                    src_ref=src.at[yo], dst_ref=dst, send_sem=beg_s.at[t * SP + yo], recv_sem=beg_r.at[my_group],
-                    device_id=(block * TG + t, yo), device_id_type=MESH,
-                ).start()
-
-            @pl.when(here)
-            def _():
-                pltpu.make_async_copy(src.at[yo], dst, beg_r.at[my_group]).start()
-
-    def give(t):
-        give_edges(t)
+            hand(eo.at[i, t * SP + yo], redge.at[:, :, :, my_lanes(i)], ret_s, ret_r, t, yo)
 
         @pl.when(jnp.logical_and(lax.rem(t, 2) == 1, t < TG - 1))
         def _():
-            give_begin(t + 1, cs.at[pl.ds(t * SP, SP)])
-
-    def carry():
-        ends = ((cs.at[pl.ds((TG - 1) * SP, SP)], cin), (chalo_src, chalo))
+            give_begin(i, t + 1, cs.at[i, pl.ds(t * SP, SP)])
+
+    def carry(i):
+        ends = ((cs.at[i, pl.ds((TG - 1) * SP, SP)], cin.at[i]), (chalo_src.at[i], chalo.at[i]))
         return [
             pltpu.make_async_remote_copy(
-                src_ref=src, dst_ref=dst, send_sem=c_s.at[i], recv_sem=c_r.at[i],
+                src_ref=src, dst_ref=dst, send_sem=c_s.at[i, e], recv_sem=c_r.at[i, e],
                 device_id=(lax.rem(p + TG, T), y), device_id_type=MESH,
             )
-            for i, (src, dst) in enumerate(ends)
+            for e, (src, dst) in enumerate(ends)
         ]
 
     def unpack(tile, f):
         return pltpu.roll(tile, LANES - 2 * hw * (f % per), 1) if f % per else tile
 
-    def whole(ref, sem):
-        pltpu.make_async_copy(ref, ref, sem).wait()
-
     R = SP * RL
 
     @pl.when(is_owner)
     def _():
         whole(dep, dep_r)
 
-        ring = W // LANES + 1
         tall = lax.broadcasted_iota(jnp.int32, (R, LANES), 1)
-
-        def turn(t, carried):
-            whole(main.at[t], a2a_r.at[0, t])
-            whole(halo.at[t], a2a_r.at[1, t])
-            cur = [[state[f, :, lanes_of(j)] for f in range(3)] for j in range(ring)]
+        slots = lax.rem(tall + hw, LANES) // (2 * hw)
+
+        def beside(block_of, outer, i):
+            if NS == 1:
+                return outer()
+            after = block_of(i + 1) if i < NS - 1 else outer()
+            before = block_of(i - 1) if i > 0 else outer()
+            return jnp.where(tall < LANES // 2, after, before)
+
+        def turn(i, t, carried):
+            if i == 0:
+                whole(main.at[t], a2a_r.at[0, t])
+                whole(halo.at[t], a2a_r.at[1, t])
+            cur = [[state[i, f, :, lanes_of(j)] for f in range(3)] for j in range(2)]
+            depths = [dep[:, lanes_of(i)], beside(lambda m: dep[:, lanes_of(m)], lambda: dep[:, W:], i)]
 
             def load(j):
-                sent = [main[t, f, :, lanes_of(j)] if j < ring - 1 else unpack(halo[t, f // per], f) for f in range(3)]
-                return [cur[j][f] + sent[f] for f in range(3)], dep[:, lanes_of(j)]
+                if j == 0:
+                    sent = [main[t, f, :, lanes_of(i)] for f in range(3)]
+                else:
+                    sent = [
+                        beside(lambda m: main[t, f, :, lanes_of(m)], lambda: unpack(halo[t, f // per], f), i)
+                        for f in range(3)
+                    ]
+                return [cur[j][f] + sent[f] for f in range(3)], depths[j]
 
             def visit(j, before, tile, after):
                 for f in range(3):
                     value = cur[j][f] + (
                         column_sum(before, tile, after, f, tall) + shift_up(tile.ups[f]) + shift_down(tile.downs[f])
                     )
-                    state[f, :, lanes_of(j)] = value
-                    if j < ring - 1:
+                    state[i, f, :, lanes_of(j)] = value
+                    if j == 0:
                         for yo in range(SP):
-                            cs[t * SP + yo, f, :, lanes_of(j)] = value[yo * RL : (yo + 1) * RL]
+                            cs[i, t * SP + yo, f] = value[yo * RL : (yo + 1) * RL]
                             below, above = (yo + 1) * RL % R, (yo * RL - 1) % R
-                            eo[t * SP + yo, 0, f, :, lanes_of(j)] = tile.ups[f][below : below + 1]
-                            eo[t * SP + yo, 1, f, :, lanes_of(j)] = tile.downs[f][above : above + 1]
-
-            walk(load, range(ring), ring, visit)
+                            eo[i, t * SP + yo, 0, f] = tile.ups[f][below : below + 1]
+                            eo[i, t * SP + yo, 1, f] = tile.downs[f][above : above + 1]
+
+            walk(load, range(2), 2, visit)
 
             @pl.when(jnp.logical_and(t > 0, block == NG - 1))
             def _():
-                give(t - 1)
+                give(i, t - 1)
 
             return carried
 
         @pl.when(block == 0)
         def _():
             whole(ini, ini_r)
-            state[...] = ini[...]
-
-        @pl.when(block > 0)
-        def _():
-            for copy in carry():
-                copy.wait_recv()
-            give_begin(0, cin)
-            for f in range(3):
-                for yo in range(SP):
-                    state[f, yo * RL : (yo + 1) * RL, :W] = cin[yo, f]
-                state[f, :, W:] = unpack(chalo[f // per], f)
-
-        lax.fori_loop(0, TG, turn, 0)
-
-        @pl.when(block == NG - 1)
-        def _():
-            give(TG - 1)
+            for i in range(NS):
+                for f in range(3):
+                    state[i, f, :, :LANES] = ini[f, :, lanes_of(i)]
+                    state[i, f, :, LANES:] = beside(lambda m: ini[f, :, lanes_of(m)], lambda: ini[f, :, W:], i)
+
+        for i in range(NS):
+            @pl.when(block > 0)
+            def _():
+                for copy in carry(i):
+                    copy.wait_recv()
+                give_begin(i, 0, cin.at[i])
+                for f in range(3):
+                    for yo in range(SP):
+                        state[i, f, yo * RL : (yo + 1) * RL, :LANES] = cin[i, yo, f]
+                    state[i, f, :, LANES:] = unpack(chalo[i, f // per], f)
+
+            lax.fori_loop(0, TG, functools.partial(turn, i), 0)
+
+            @pl.when(block == NG - 1)
+            def _():
+                give(i, TG - 1)
+
+            @pl.when(block < NG - 1)
+            def _():
+                for e in range(nh):
+                    packed = jnp.zeros((R, LANES), jnp.float32)
+                    for f in range(e * per, min(3, (e + 1) * per)):
+                        z = state[i, f, :, LANES:]
+                        if f % per:
+                            z = pltpu.roll(z, 2 * hw * (f % per), 1)
+                        packed = jnp.where(slots == f % per, z, packed)
+                    chalo_src[i, e] = packed
+                if i == 0:
+                    pl.semaphore_wait(go_carry, 1)
+                for copy in carry(i):
+                    copy.start()
 
         @pl.when(block < NG - 1)
         def _():
-            lanes = lax.broadcasted_iota(jnp.int32, (SP * RL, LANES), 1)
-            slots = lax.rem(lanes + hw, LANES) // (2 * hw)
-            for i in range(nh):
-                packed = jnp.zeros((SP * RL, LANES), jnp.float32)
-                for f in range(i * per, min(3, (i + 1) * per)):
-                    z = state[f, :, W:]
-                    if f % per:
-                        z = pltpu.roll(z, 2 * hw * (f % per), 1)
-                    packed = jnp.where(slots == f % per, z, packed)
-                chalo_src[i] = packed
-            pl.semaphore_wait(go_carry, 1)
-            for copy in carry():
-                copy.start()
-
             @pl.loop(0, TG)
             def _(t):
-                give(t)
-
-    width, part = NX // GROUPS, NX // PARTS
+                for i in range(NS):
+                    give(i, t)
+
+    part = NX // PARTS
 
     def fwd(q):
         cols = pl.ds(q * part, part)
         return pltpu.make_async_remote_copy(
             src_ref=ce.at[:, :, cols], dst_ref=cb.at[:, :, cols],
-            send_sem=fwd_s.at[q], recv_sem=fwd_r.at[q], device_id=(lax.rem(p + 1, T), y), device_id_type=MESH,
-        )
-
-    for q in range(GROUPS):
-        whole(redge.at[:, :, :, pl.ds(q * width, width)], ret_r.at[q])
+            send_sem=fwd_s, recv_sem=fwd_r.at[q], device_id=(lax.rem(p + 1, T), y), device_id_type=MESH,
+        )
+
+    whole(redge, ret_r)
 
     @pl.when(p == 0)
     def _():
@@ -647,8 +671,7 @@
 
     @pl.when(late)
     def _():
-        for q in range(GROUPS):
-            whole(cb.at[:, :, pl.ds(q * width, width)], beg_r.at[q])
+        whole(cb, beg_r)
 
     per_part = NT // PARTS
 
@@ -688,8 +711,7 @@
             fwd(q).start()
         for j in range(NT):
             emit(lanes_of(j), [ce[f, :, lanes_of(j)] for f in range(3)])
-        for q in order:
-            fwd(q).wait_send()
+        whole(ce, fwd_s)
 
     @pl.when(odd)
     def _():
@@ -702,20 +724,15 @@
 
     @pl.when(p < T - 1)
     def _():
-        for c in range(NC):
-            shift(c, w).wait_send()
+        whole(u_ref.at[2], shift_s)
 
     @pl.when(late)
     def _():
         for side in range(sides):
             depth_halo(side).wait_send()
-            for c in range(NC):
-                relay(c, side).wait_send()
-
-    for stage in range(2):
-        for side in range(2):
-            for part in range(SPANS):
-                edge_copy(stage, side, part).wait_send()
+            whole(rsrc, rel_s.at[side])
+
+    whole(esrc, edge_s)
     for yo in range(SP):
         flat = pb * SP + yo
 
@@ -731,22 +748,22 @@
     def _():
         whole(b.at[:, :, pl.ds(0, (K - 1) * W)], a2a_s.at[0])
         whole(halo_src.at[:, :, pl.ds(0, (K - 1) * LANES)], a2a_s.at[1])
-        whole(eo.at[pl.ds(0, TG * SP - 1)], ret_s)
+        for i in range(NS):
+            whole(eo.at[i, pl.ds(0, TG * SP - 1)], ret_s)
 
         @pl.when(block < NG - 1)
         def _():
-            for copy in carry():
-                copy.wait_send()
-
-        for t in range(0, TG, 2):
-            for yo in range(SP):
-                sent = jnp.logical_not(jnp.logical_and(t == pb, y == yo))
-                if t == 0:
-                    sent = jnp.logical_and(sent, block > 0)
-
-                @pl.when(sent)
-                def _():
-                    pltpu.make_async_copy(cin.at[yo], cin.at[yo], beg_s.at[t * SP + yo]).wait()
+            for i in range(NS):
+                for copy in carry(i):
+                    copy.wait_send()
+
+        own = jnp.logical_and(even, p > 0).astype(jnp.int32)
+        begins = (TG + 1) // 2 * SP - own - jnp.where(block == 0, SP, 0)
+        for n in ((TG + 1) // 2 * SP - a - c for a in range(2) for c in (0, SP)):
+            @pl.when(begins == n)
+            def _():
+                for i in range(NS):
+                    whole(cs.at[i, pl.ds(0, n)], beg_s)
 
     @pl.when(jnp.logical_not(is_owner))
     def _():
@@ -796,19 +813,19 @@
                 pltpu.VMEM((3, R, W + LANES), f32),
                 pltpu.VMEM((T // NG, 3, R, W), f32),
                 pltpu.VMEM((T // NG, nh, R, LANES), f32),
-                pltpu.VMEM((members, 3, RL, W), f32),
+                pltpu.VMEM((W // LANES, members, 3, RL, LANES), f32),
                 state, state,
                 edges, edges,
-                pltpu.VMEM((members, 2, 3, 1, W), f32),
+                pltpu.VMEM((W // LANES, members, 2, 3, 1, LANES), f32),
                 pltpu.VMEM((2, 3, 1, NX), f32),
-                pltpu.VMEM((SP, 3, RL, W), f32),
-                pltpu.VMEM((nh, R, LANES), f32),
-                pltpu.VMEM((nh, R, LANES), f32),
-                pltpu.VMEM((3, R, W + LANES), f32),
-                dma((NC,)), dma((NC,)), dma((sides, NC)), dma((sides, NC)), dma((sides,)), dma((sides,)),
-                dma((2, 2, SPANS)), dma((2, 2, SPANS)), dma((SP,)), dma, dma((SP,)), dma, dma((2,)), dma((2, T // NG)),
-                dma, dma((GROUPS,)), dma((PARTS,)), dma((PARTS,)),
-                dma((2,)), dma((2,)), dma((members,)), dma((GROUPS,)), dma((5,)),
+                pltpu.VMEM((W // LANES, SP, 3, RL, LANES), f32),
+                pltpu.VMEM((W // LANES, nh, R, LANES), f32),
+                pltpu.VMEM((W // LANES, nh, R, LANES), f32),
+                pltpu.VMEM((W // LANES, 3, R, 2 * LANES), f32),
+                dma, dma((NC,)), dma((sides,)), dma((sides, NC)), dma((sides,)), dma((sides,)),
+                dma, dma((2, SPANS)), dma((SP,)), dma, dma((SP,)), dma, dma((2,)), dma((2, T // NG)),
+                dma, dma, dma, dma((PARTS,)),
+                dma((W // LANES, 2)), dma((W // LANES, 2)), dma, dma, dma((5,)),
                 pltpu.SemaphoreType.REGULAR,
             ],
             compiler_params=pltpu.CompilerParams(

time: 45.4 us -> 44 us (0.969)
  Pallas kernels: 43.6 us -> 41.9 us
    pallas_call x1, Pallas kernels: 43.6 us -> 41.9 us  [per_device(): pl.pallas_call(functools.partial(kernel, cfg), out_shape=pltpu.VMEM(fine_...]
where the time goes in v5:
time: 44 us; the launch traced here: 43.3 us
  Pallas kernels  41.9 us (95%)
  local copies, waits for them, and re-layouts  1.41 us (3%)
    pallas_call x1, Pallas kernels, per_device(): pl.pallas_call(functools.partial(kernel, cfg), out_shape=pltpu.VMEM(fine_...  41.9 us
    unnamed x1, local copies, waits for them, and re-layouts  1.41 us

profile of v5, /device:TPU:27, one launch (start us, length us, event | category | flops | bytes accessed | tf_op | source)
XLA Modules:
  0.0 43.3 jit_solution(15267121431506317405)
XLA Ops:
  0.0 41.9 %shard_map.37 = f32[1,3,3,16,4096]{4,3,2,1,0:T(8,128)S(1)} custom-call(f32[1,3,3,16,4096]{4,3,2,1,0:T(8,128)} %u_hbm.1, f32[3,16,4096]{2,1,0:T(8,128)} %init_hbm.1, f32[16,4096]{1,0:T(8,128)} %depth_hbm.1), custom_call_target="tpu_custom_call" | custom-call | tf_op jit(solution)/shard_map/pallas_call | solution.py:797
  41.9 1.4 %copy.5 = f32[1,3,3,16,4096]{4,3,2,1,0:T(8,128)} copy(f32[1,3,3,16,4096]{4,3,2,1,0:T(8,128)S(1)} %shard_map.37) | data formatting | bytes 4718592

commit v6 on v5

--- a/solution.py
+++ b/solution.py
@@ -103,7 +103,8 @@
     shift_s, shift_r, rel_s, rel_r, dh_s, dh_r, edge_s, edge_r, dep_s, dep_r, ini_s, ini_r, a2a_s, a2a_r, ret_s, ret_r,
     fwd_s, fwd_r, c_s, c_r, beg_s, beg_r, in_s, go_carry,
 ):
-    T, SP, RL, NX, W, K, stride, hw, per, nh, NG, NC = cfg
+    T, SP, RL, NX, W, K, stride, hw, per, nh, NG, NC, carry_hw = cfg
+    carry_slots = LANES // (2 * carry_hw)
     TG = T // NG
     WC = NX // NC
     tpc = K // NC
@@ -560,7 +561,8 @@
         whole(dep, dep_r)
 
         tall = lax.broadcasted_iota(jnp.int32, (R, LANES), 1)
-        slots = lax.rem(tall + hw, LANES) // (2 * hw)
+        half = lax.broadcasted_iota(jnp.int32, (R // 2, LANES), 1)
+        slots = lax.rem(half + carry_hw, LANES) // (2 * carry_hw)
 
         def beside(block_of, outer, i):
             if NS == 1:
@@ -624,7 +626,12 @@
                 for f in range(3):
                     for yo in range(SP):
                         state[i, f, yo * RL : (yo + 1) * RL, :LANES] = cin[i, yo, f]
-                    state[i, f, :, LANES:] = unpack(chalo[i, f // per], f)
+                    for r in range(2):
+                        slot = 2 * f + r
+                        tile = chalo[i, slot // carry_slots]
+                        if slot % carry_slots:
+                            tile = pltpu.roll(tile, LANES - 2 * carry_hw * (slot % carry_slots), 1)
+                        state[i, f, r * R // 2 : (r + 1) * R // 2, LANES:] = tile
 
             lax.fori_loop(0, TG, functools.partial(turn, i), 0)
 
@@ -634,13 +641,14 @@
 
             @pl.when(block < NG - 1)
             def _():
-                for e in range(nh):
-                    packed = jnp.zeros((R, LANES), jnp.float32)
-                    for f in range(e * per, min(3, (e + 1) * per)):
-                        z = state[i, f, :, LANES:]
-                        if f % per:
-                            z = pltpu.roll(z, 2 * hw * (f % per), 1)
-                        packed = jnp.where(slots == f % per, z, packed)
+                for e in range(chalo.shape[1]):
+                    packed = jnp.zeros((R // 2, LANES), jnp.float32)
+                    for slot in range(e * carry_slots, min(6, (e + 1) * carry_slots)):
+                        f, r = slot // 2, slot % 2
+                        z = state[i, f, r * R // 2 : (r + 1) * R // 2, LANES:]
+                        if slot % carry_slots:
+                            z = pltpu.roll(z, 2 * carry_hw * (slot % carry_slots), 1)
+                        packed = jnp.where(slots == slot % carry_slots, z, packed)
                     chalo_src[i, e] = packed
                 if i == 0:
                     pl.semaphore_wait(go_carry, 1)
@@ -787,7 +795,11 @@
             hw *= 2
         per = LANES // (2 * hw)
         nh = -(-3 // per)
-        cfg = (T, SP, RL, NX, W, K, stride, hw, per, nh, NG, NC)
+        carry_hw = 8
+        while carry_hw < T // NG:
+            carry_hw *= 2
+        carried = -(-6 * 2 * carry_hw // LANES)
+        cfg = (T, SP, RL, NX, W, K, stride, hw, per, nh, NG, NC, carry_hw)
         f32, dma = jnp.float32, pltpu.SemaphoreType.DMA
         state = pltpu.VMEM((3, RL, NX), f32)
         R = RL * SP
@@ -819,8 +831,8 @@
                 pltpu.VMEM((W // LANES, members, 2, 3, 1, LANES), f32),
                 pltpu.VMEM((2, 3, 1, NX), f32),
                 pltpu.VMEM((W // LANES, SP, 3, RL, LANES), f32),
-                pltpu.VMEM((W // LANES, nh, R, LANES), f32),
-                pltpu.VMEM((W // LANES, nh, R, LANES), f32),
+                pltpu.VMEM((W // LANES, carried, R // 2, LANES), f32),
+                pltpu.VMEM((W // LANES, carried, R // 2, LANES), f32),
                 pltpu.VMEM((W // LANES, 3, R, 2 * LANES), f32),
                 dma, dma((NC,)), dma((sides,)), dma((sides, NC)), dma((sides,)), dma((sides,)),
                 dma, dma((2, SPANS)), dma((SP,)), dma, dma((SP,)), dma, dma((2,)), dma((2, T // NG)),

time: 44 us -> 43.4 us (0.986)
  no operation moved by 1% of the time
where the time goes in v6:
time: 43.4 us; the launch traced here: 42.9 us
  Pallas kernels  41.5 us (96%)
  local copies, waits for them, and re-layouts  1.41 us (3%)
    pallas_call x1, Pallas kernels, per_device(): pl.pallas_call(functools.partial(kernel, cfg), out_shape=pltpu.VMEM(fine_...  41.5 us
    unnamed x1, local copies, waits for them, and re-layouts  1.41 us

profile of v6, /device:TPU:27, one launch (start us, length us, event | category | flops | bytes accessed | tf_op | source)
XLA Modules:
  0.0 42.9 jit_solution(18331072345081782212)
XLA Ops:
  0.0 41.5 %shard_map.37 = f32[1,3,3,16,4096]{4,3,2,1,0:T(8,128)S(1)} custom-call(f32[1,3,3,16,4096]{4,3,2,1,0:T(8,128)} %u_hbm.1, f32[3,16,4096]{2,1,0:T(8,128)} %init_hbm.1, f32[16,4096]{1,0:T(8,128)} %depth_hbm.1), custom_call_target="tpu_custom_call" | custom-call | tf_op jit(solution)/shard_map/pallas_call | solution.py:809
  41.5 1.4 %copy.5 = f32[1,3,3,16,4096]{4,3,2,1,0:T(8,128)} copy(f32[1,3,3,16,4096]{4,3,2,1,0:T(8,128)S(1)} %shard_map.37) | data formatting | bytes 4718592

commit v7 on v6

--- a/solution.py
+++ b/solution.py
@@ -142,8 +142,15 @@
     has_next, has_last = block < NG - 1, block > 0
     crosses = jnp.logical_and(has_next, pb == TG - 1)
 
+    first_of_block = jnp.logical_and(has_last, pb == 0)
+    meets = jnp.logical_or(crosses, first_of_block)
+
     def announce(sem, pp):
         pl.semaphore_signal(sem, inc=1, device_id=(pp, y), device_id_type=MESH)
+
+    @pl.when(first_of_block)
+    def _():
+        announce(barrier, lax.rem(p + T - 1, T))
 
     @pl.loop(1, members)
     def _(i):
@@ -165,13 +172,6 @@
     for copy in loads:
         copy.start()
     loads[0].wait()
-    first_of_block = jnp.logical_and(has_last, pb == 0)
-    meets = jnp.logical_or(crosses, first_of_block)
-
-    @pl.when(first_of_block)
-    def _():
-        announce(barrier, lax.rem(p + T - 1, T))
-
     pl.semaphore_wait(barrier, members - 1 + has_last.astype(jnp.int32) + meets.astype(jnp.int32))
 
     @pl.when(has_last)

time: 43.4 us -> 43.4 us (level)
  no operation moved by 1% of the time
where the time goes in v7:
time: 43.4 us; the launch traced here: 42.9 us
  Pallas kernels  41.5 us (96%)
  local copies, waits for them, and re-layouts  1.41 us (3%)
    pallas_call x1, Pallas kernels, per_device(): pl.pallas_call(functools.partial(kernel, cfg), out_shape=pltpu.VMEM(fine_...  41.5 us
    unnamed x1, local copies, waits for them, and re-layouts  1.41 us

profile of v7, /device:TPU:27, one launch (start us, length us, event | category | flops | bytes accessed | tf_op | source)
XLA Modules:
  0.0 42.9 jit_solution(986238775092859352)
XLA Ops:
  0.0 41.5 %shard_map.37 = f32[1,3,3,16,4096]{4,3,2,1,0:T(8,128)S(1)} custom-call(f32[1,3,3,16,4096]{4,3,2,1,0:T(8,128)} %u_hbm.1, f32[3,16,4096]{2,1,0:T(8,128)} %init_hbm.1, f32[16,4096]{1,0:T(8,128)} %depth_hbm.1), custom_call_target="tpu_custom_call" | custom-call | tf_op jit(solution)/shard_map/pallas_call | solution.py:809
  41.5 1.4 %copy.5 = f32[1,3,3,16,4096]{4,3,2,1,0:T(8,128)} copy(f32[1,3,3,16,4096]{4,3,2,1,0:T(8,128)S(1)} %shard_map.37) | data formatting | bytes 4718592
